TPU v7x, 32 devices: a whole 2x2x4 slice. The times are simulated.
32 devices in a mesh: grp: 2 (over y), lat: 4 (over z), lon: 2 (over x), ch: 2 (over core).
Axes of the slice: x: 2, y: 2, z: 4, core: 2. Of those that a mesh axis runs over, the one named last changes fastest.
Arguments:
- noisy_state: bfloat16 [256, 32, 512], P(('grp', 'ch'), 'lat', 'lon'), parts along dimension 0, may hold values from -6 to 6
- kernel_in: bfloat16 [3, 3, 128, 128], replicated, may hold values from -0.1875 to 0.1875
- bias_in: float32 [128], replicated, may hold values from -4 to 4
- kernel_out: bfloat16 [3, 3, 128, 128], replicated, may hold values from -0.1875 to 0.1875
- interp_weight: bfloat16 [64, 128, 128], P(('grp', 'lat', 'lon')), parts along dimension 0, may hold values from -0.5 to 0.5
- observed: bfloat16 [64, 128, 128], P(('grp', 'lat', 'lon'), 'ch'), parts along dimension 0, may hold values from -6 to 6
- obs_precision: bfloat16 [64, 128], P(('grp', 'lat', 'lon')), parts along dimension 0, may hold values from 0.29882812 to 3
- dest_tile: int32 [64], P(('grp', 'lat', 'lon')), parts along dimension 0, may hold values from 0 to 3, as said below
- row_offset: int32 [64], P(('grp', 'lat', 'lon')), parts along dimension 0, may hold values from 0 to 4
- col_offset: int32 [64], P(('grp', 'lat', 'lon')), parts along dimension 0, may hold values from 0 to 224
Outputs:
- next_state: float32 [256, 32, 512], P(('grp', 'ch'), 'lat', 'lon'), parts along dimension 0
- innovation: bfloat16 [64, 128, 128], P(('grp', 'lat', 'lon'), 'ch'), parts along dimension 0
There are 2 independent parts, one for each index of `grp`. A program takes and returns all parts, laid end to end along the dimension named above; an argument that names none is the same for every part. Nothing has to cross between parts.
Inputs may be any that keep to these rules, and one draw needn't show every extreme that they name: `dest_tile`: the 4 blocks of one device name any one latitude tile at most 2 times; a block's tile lies in the longitude column of the device that holds the block.
All inputs are finite; a program needn't handle non-finite values.
Results may differ from a plain program's by a relative error of at most 0.0085.
Values may be sent and summed in bfloat16 or wider, within the bound.
A program may use at most 64 MiB of HBM per device.

v0:
```python
import jax
import jax.numpy as jnp
from jax import lax
from jax.sharding import PartitionSpec as P

OBS = 128
PH = 4
PW = 32
CAP = 2


keep_rate = 0.6
blend_rate = 0.4
guide_rate = 0.3


def extended(shard, sides, width):
    for axis, dim in sides:
        size, length = (lax.axis_size(axis), shard.shape[dim])
        up = [(i, (i + 1) % size) for i in range(size)]
        down = [(j, i) for i, j in up]
        last = lax.slice_in_dim(shard, length - width, length, axis=dim)
        initial = lax.slice_in_dim(shard, 0, width, axis=dim)
        before = lax.ppermute(last, axis, up)
        after = lax.ppermute(initial, axis, down)
        shard = jnp.concatenate([before, shard, after], axis=dim)
    return shard


def with_rims(grid_field):
    padded = extended(grid_field, (("lat", 1), ("lon", 2)), 1)
    position = lax.axis_index("lat")
    lat_count = lax.axis_size("lat")
    levels = lax.broadcasted_iota(jnp.int32, (1, padded.shape[1], 1), 1)
    inside = ((levels > 0) | (position > 0)) & (
        (levels < padded.shape[1] - 1) | (position < lat_count - 1)
    )
    return jnp.where(inside, padded, jnp.zeros((), padded.dtype))


def apply_taps(running, kernel_part, padded, grid_rows, grid_cols):
    in_count = padded.shape[0]
    out_count = kernel_part.shape[2]
    for tap_row in range(3):
        stacked = jnp.concatenate(
            [
                padded[:, tap_row : tap_row + grid_rows, tap_col : tap_col + grid_cols]
                for tap_col in range(3)
            ],
            axis=0,
        )
        row_kernel = jnp.transpose(kernel_part[tap_row], (1, 0, 2)).reshape(out_count, 3 * in_count)
        running = running + jnp.einsum(
            "oi,ihw->ohw", row_kernel, stacked, preferred_element_type=jnp.float32
        )
    return running


def convolve(grid_field, kernel_rows):
    padded = with_rims(grid_field)
    grid_rows, grid_cols = (grid_field.shape[1], grid_field.shape[2])
    initial = jnp.zeros((kernel_rows.shape[2], grid_rows, grid_cols), jnp.float32)
    return apply_taps(
        initial, kernel_rows, lax.all_gather(padded, "ch", axis=0, tiled=True), grid_rows, grid_cols
    )


def forward_rows(kernel, first_channel, own_channels):
    return lax.dynamic_slice_in_dim(kernel, first_channel, own_channels, 2)


def adjoint_rows(kernel, first_channel, own_channels):
    columns = lax.dynamic_slice_in_dim(kernel, first_channel, own_channels, 3)
    return jnp.transpose(columns[::-1, ::-1], (0, 1, 3, 2))


def extract(grid_field, patch_rows, patch_cols):

    def take_one(row_start, col_start):
        return lax.dynamic_slice(
            grid_field,
            (jnp.zeros((), jnp.int32), row_start, col_start),
            (grid_field.shape[0], PH, PW),
        )

    return jax.vmap(take_one)(patch_rows, patch_cols)


def spread(grad_patch, patch_rows, patch_cols, grid_shape):
    cell_rows = patch_rows[:, None, None] + lax.broadcasted_iota(jnp.int32, (1, PH, 1), 1)
    cell_cols = patch_cols[:, None, None] + lax.broadcasted_iota(jnp.int32, (1, 1, PW), 2)
    return (
        jnp.zeros(grid_shape, jnp.float32)
        .at[:, cell_rows, cell_cols]
        .add(jnp.moveaxis(grad_patch, 1, 0))
    )


def slot_plan(dest_tile, lat_tiles):
    blocks = dest_tile.shape[0]
    matches = (dest_tile[:, None] == lax.broadcasted_iota(jnp.int32, (1, lat_tiles), 1)).astype(
        jnp.int32
    )
    before = jnp.cumsum(matches, axis=0) - matches
    slot_rank = jnp.sum(before * matches, axis=1)
    flat_slot = dest_tile * CAP + slot_rank
    filler = (
        jnp.full((lat_tiles * CAP,), blocks, jnp.int32)
        .at[flat_slot]
        .set(lax.iota(jnp.int32, blocks))
    )
    filled = filler < blocks
    source = jnp.minimum(filler, blocks - 1)
    return (flat_slot, source, filled)


def observe(denoised, interp_weight, observed, obs_precision, dest_tile, row_offset, col_offset):
    own_channels = denoised.shape[0]
    grid_shape = denoised.shape
    lat_tiles = lax.axis_size("lat")
    slots = lat_tiles * CAP
    flat_slot, source, filled = slot_plan(dest_tile, lat_tiles)
    rows_out = row_offset[source].reshape(lat_tiles, CAP)
    cols_out = col_offset[source].reshape(lat_tiles, CAP)
    weights_out = jnp.where(
        filled[:, None, None], interp_weight[source], jnp.zeros((), jnp.bfloat16)
    ).reshape(lat_tiles, CAP, OBS, PH * PW)
    values_out = observed[source].reshape(lat_tiles, CAP, own_channels, OBS)
    scale_out = jnp.where(
        filled[:, None], obs_precision[source], jnp.zeros((), jnp.bfloat16)
    ).reshape(lat_tiles, CAP, OBS)
    arrived = (
        lax.all_to_all(weights_out, "lat", split_axis=0, concat_axis=0, tiled=True),
        lax.all_to_all(values_out, "lat", split_axis=0, concat_axis=0, tiled=True),
        lax.all_to_all(scale_out, "lat", split_axis=0, concat_axis=0, tiled=True),
        lax.all_to_all(rows_out, "lat", split_axis=0, concat_axis=0, tiled=True),
        lax.all_to_all(cols_out, "lat", split_axis=0, concat_axis=0, tiled=True),
    )
    weights_in = arrived[0].reshape(slots, OBS, PH * PW)
    values_in = arrived[1].reshape(slots, own_channels, OBS)
    scale_in = arrived[2].reshape(slots, OBS)
    rows_in = arrived[3].reshape(slots)
    cols_in = arrived[4].reshape(slots)
    patches = extract(denoised, rows_in, cols_in).reshape(slots, own_channels, PH * PW)
    predicted = jnp.einsum("scp,sop->sco", patches, weights_in, preferred_element_type=jnp.float32)
    residual = predicted - values_in.astype(jnp.float32)
    rounded = residual.astype(jnp.bfloat16).reshape(lat_tiles, CAP, own_channels, OBS)
    returned = lax.all_to_all(rounded, "lat", split_axis=0, concat_axis=0, tiled=True).reshape(
        slots, own_channels, OBS
    )
    innovation = returned[flat_slot]
    weighted = (residual * scale_in.astype(jnp.float32)[:, None, :]).astype(jnp.bfloat16)
    pulled = jnp.einsum("sco,sop->scp", weighted, weights_in, preferred_element_type=jnp.float32)
    grad_field = spread(pulled.reshape(slots, own_channels, PH, PW), rows_in, cols_in, grid_shape)
    return (grad_field, innovation)


def body(
    noisy_state,
    kernel_in,
    bias_in,
    kernel_out,
    interp_weight,
    observed,
    obs_precision,
    dest_tile,
    row_offset,
    col_offset,
):
    own_channels = noisy_state.shape[0]
    first_channel = lax.axis_index("ch") * own_channels
    bias_local = lax.dynamic_slice_in_dim(bias_in, first_channel, own_channels, 0)
    pre_act = (
        convolve(noisy_state, forward_rows(kernel_in, first_channel, own_channels))
        + bias_local[:, None, None]
    )
    hidden = jax.nn.silu(pre_act).astype(jnp.bfloat16)
    denoised = (
        noisy_state.astype(jnp.float32)
        + convolve(hidden, forward_rows(kernel_out, first_channel, own_channels))
    ).astype(jnp.bfloat16)
    grad_field, innovation = observe(
        denoised, interp_weight, observed, obs_precision, dest_tile, row_offset, col_offset
    )
    grad_round = grad_field.astype(jnp.bfloat16)
    back_hidden = convolve(grad_round, adjoint_rows(kernel_out, first_channel, own_channels))
    sigmoid_act = jax.nn.sigmoid(pre_act)
    grad_pre = (back_hidden * sigmoid_act * (1.0 + pre_act * (1.0 - sigmoid_act))).astype(
        jnp.bfloat16
    )
    grad_state = grad_field + convolve(
        grad_pre, adjoint_rows(kernel_in, first_channel, own_channels)
    )
    next_state = (
        keep_rate * noisy_state.astype(jnp.float32)
        + blend_rate * denoised.astype(jnp.float32)
        - guide_rate * grad_state
    )
    return (next_state, innovation)


def solution(mesh):
    return jax.shard_map(
        body,
        mesh=mesh,
        in_specs=(
            P(("grp", "ch"), "lat", "lon"),
            P(),
            P(),
            P(),
            P(("grp", "lat", "lon"), None, None),
            P(("grp", "lat", "lon"), "ch", None),
            P(("grp", "lat", "lon"), None),
            P(("grp", "lat", "lon")),
            P(("grp", "lat", "lon")),
            P(("grp", "lat", "lon")),
        ),
        out_specs=(P(("grp", "ch"), "lat", "lon"), P(("grp", "lat", "lon"), "ch", None)),
        check_vma=False,
    )
```

profile of v0, /device:TPU:0, one launch (start us, length us, event | category | flops | bytes accessed | tf_op | source)
XLA Modules:
  0.0 143.8 jit_solution(14844164952837276044)
XLA Ops:
  0.7 1.2 fusion.163
  1.9 3.1 %collective-permute-start = (bf16[64,1,256]{2,0,1:T(8,128)(2,1)S(1)}, bf16[64,1,256]{2,0,1:T(8,128)(2,1)S(1)}, u32[]{:S(2)}, u32[]{:S(2)}) collective-permute-start(bf16[64,1,256]{2,0,1:T(8,128)(2,1)S(1)} %copy.179), channel_id=1, source_target_pairs={{0,4},{4,8},{8,12},{12,0},{1,5},{5,9},{9,13},{13,1},{2,6},{6,10},{... | collective-permute-start | bytes 98312 | tf_op jit(solution)/shard_map/ppermute | solution.py:24
  5.0 2.1 %collective-permute-start.1 = (bf16[64,1,256]{2,0,1:T(8,128)(2,1)S(1)}, bf16[64,1,256]{2,0,1:T(8,128)(2,1)S(1)}, u32[]{:S(2)}, u32[]{:S(2)}) collective-permute-start(bf16[64,1,256]{2,0,1:T(8,128)(2,1)S(1)} %copy.180), channel_id=1, source_target_pairs={{4,0},{8,4},{12,8},{0,12},{5,1},{9,5},{13,9},{1,13},{6,2},{10,6},{... | collective-permute-start | bytes 98312 | tf_op jit(solution)/shard_map/ppermute | solution.py:25
  7.1 0.7 fusion.134
  7.9 0.8 select_reduce_fusion
  8.7 0.7 compare_select_fusion.5
  10.0 1.3 gather_fusion.1
  11.3 0.7 all_to_all.26
  12.0 3.2 %all-to-all-start.1 = ((s32[4,1,2]{2,1,0:T(1,128)}), s32[4,1,2]{2,1,0:T(1,128)S(1)}, u32[]{:S(2)}, u32[]{:S(2)}) async-start(s32[4,1,2]{2,1,0:T(1,128)} %bitcast.13), calls=%async_computation.1 | async-start | bytes 4096 | tf_op jit(solution)/shard_map/all_to_all | solution.py:137
  16.3 0.6 gather_fusion
  17.0 0.7 all_to_all.24
  18.3 1.2 gather_fusion.3
  20.1 0.8 broadcast_select_fusion
  20.9 0.7 broadcast_select_fusion.2
  21.6 5.1 %all-to-all-start = ((s32[4,1,2]{2,1,0:T(1,128)}), s32[4,1,2]{2,1,0:T(1,128)S(1)}, u32[]{:S(2)}, u32[]{:S(2)}) async-start(s32[4,1,2]{2,1,0:T(1,128)} %bitcast.12), calls=%async_computation | async-start | bytes 4096 | tf_op jit(solution)/shard_map/all_to_all | solution.py:136
  27.2 0.7 reduce.14
  28.0 4.2 %all-to-all-done = s32[4,1,2]{2,1,0:T(1,128)S(1)} async-done(((s32[4,1,2]{2,1,0:T(1,128)}), s32[4,1,2]{2,1,0:T(1,128)S(1)}, u32[]{:S(2)}, u32[]{:S(2)}) %all-to-all-start) | async-done | bytes 64 | tf_op jit(solution)/shard_map/all_to_all | solution.py:136
  32.2 3.2 %all-to-all-start.4 = ((bf16[4,2,128]{2,1,0:T(2,128)(2,1)}), bf16[4,2,128]{2,1,0:T(2,128)(2,1)S(1)}, u32[]{:S(2)}, u32[]{:S(2)}) async-start(bf16[4,2,128]{2,1,0:T(2,128)(2,1)} %broadcast_select_fusion.2), calls=%async_computation.4 | async-start | bytes 4096 | tf_op jit(solution)/shard_map/all_to_all | solution.py:135
  35.4 0.7 reduce.15
  36.7 1.7 %collective-permute-start.2 = (bf16[64,10,1]{2,0,1:T(8,128)(2,1)S(1)}, bf16[64,10,1]{2,0,1:T(8,128)(2,1)S(1)}, u32[]{:S(2)}, u32[]{:S(2)}) collective-permute-start(bf16[64,10,1]{2,0,1:T(8,128)(2,1)S(1)} %get-tuple-element.98), channel_id=1, source_target_pairs={{0,2},{2,0},{1,3},{3,1},{4,6},{6,4},{5,7},{7,5},{8,10},{10,8},{9,1... | collective-permute-start | bytes 3848 | tf_op jit(solution)/shard_map/ppermute | solution.py:24
  38.9 3.5 %collective-permute-done.2 = bf16[64,10,1]{2,0,1:T(8,128)(2,1)S(1)} collective-permute-done((bf16[64,10,1]{2,0,1:T(8,128)(2,1)S(1)}, bf16[64,10,1]{2,0,1:T(8,128)(2,1)S(1)}, u32[]{:S(2)}, u32[]{:S(2)}) %collective-permute-start.2) | collective-permute-done | bytes 1312 | tf_op jit(solution)/shard_map/ppermute | solution.py:24
  42.4 1.8 %collective-permute-done.3 = bf16[64,10,1]{2,0,1:T(8,128)(2,1)S(1)} collective-permute-done((bf16[64,10,1]{2,0,1:T(8,128)(2,1)S(1)}, bf16[64,10,1]{2,0,1:T(8,128)(2,1)S(1)}, u32[]{:S(2)}, u32[]{:S(2)}) %collective-permute-start.3) | collective-permute-done | bytes 1312 | tf_op jit(solution)/shard_map/ppermute | solution.py:25
  44.5 2.5 %all_gather.12 = bf16[128,10,258]{2,0,1:T(8,128)(2,1)S(1)} all-gather(bf16[64,10,258]{2,0,1:T(8,128)(2,1)S(1)} %maximum_select_fusion), channel_id=1, replica_groups=mesh['grp'=2,'lat'=4,'lon'=2,'ch'=2] {'ch'}, dimensions={0}, use_global_device_ids=true | all-gather | bytes 990720 | tf_op jit(solution)/shard_map/all_gather | solution.py:64
  47.0 1.2 fusion.153
  49.0 1.2 multiply_convert_fusion
  50.2 1.7 %collective-permute-start.4 = (bf16[64,1,256]{2,0,1:T(8,128)(2,1)S(1)}, bf16[64,1,256]{2,0,1:T(8,128)(2,1)S(1)}, u32[]{:S(2)}, u32[]{:S(2)}) collective-permute-start(bf16[64,1,256]{2,0,1:T(8,128)(2,1)S(1)} %get-tuple-element.116), channel_id=1, source_target_pairs={{0,4},{4,8},{8,12},{12,0},{1,5},{5,9},{9,13},{13,1},{2,6},{6,10},{... | collective-permute-start | bytes 98312 | tf_op jit(solution)/shard_map/ppermute | solution.py:24
  51.9 2.1 %collective-permute-start.5 = (bf16[64,1,256]{2,0,1:T(8,128)(2,1)S(1)}, bf16[64,1,256]{2,0,1:T(8,128)(2,1)S(1)}, u32[]{:S(2)}, u32[]{:S(2)}) collective-permute-start(bf16[64,1,256]{2,0,1:T(8,128)(2,1)S(1)} %get-tuple-element.117), channel_id=1, source_target_pairs={{4,0},{8,4},{12,8},{0,12},{5,1},{9,5},{13,9},{1,13},{6,2},{10,6},{... | collective-permute-start | bytes 98312 | tf_op jit(solution)/shard_map/ppermute | solution.py:25
  54.1 2.0 %collective-permute-done.4 = bf16[64,1,256]{2,0,1:T(8,128)(2,1)S(1)} collective-permute-done((bf16[64,1,256]{2,0,1:T(8,128)(2,1)S(1)}, bf16[64,1,256]{2,0,1:T(8,128)(2,1)S(1)}, u32[]{:S(2)}, u32[]{:S(2)}) %collective-permute-start.4) | collective-permute-done | bytes 32800 | tf_op jit(solution)/shard_map/ppermute | solution.py:24
  56.4 1.6 %collective-permute-start.6 = (bf16[64,10,1]{2,0,1:T(8,128)(2,1)S(1)}, bf16[64,10,1]{2,0,1:T(8,128)(2,1)S(1)}, u32[]{:S(2)}, u32[]{:S(2)}) collective-permute-start(bf16[64,10,1]{2,0,1:T(8,128)(2,1)S(1)} %get-tuple-element.96), channel_id=1, source_target_pairs={{0,2},{2,0},{1,3},{3,1},{4,6},{6,4},{5,7},{7,5},{8,10},{10,8},{9,1... | collective-permute-start | bytes 3848 | tf_op jit(solution)/shard_map/ppermute | solution.py:24
  58.6 4.8 %all-to-all-start.3 = ((bf16[4,2,64,128]{3,2,1,0:T(8,128)(2,1)}), bf16[4,2,64,128]{3,2,1,0:T(8,128)(2,1)S(1)}, u32[]{:S(2)}, u32[]{:S(2)}) async-start(bf16[4,2,64,128]{3,2,1,0:T(8,128)(2,1)} %bitcast.17), calls=%async_computation.3 | async-start | bytes 262144 | tf_op jit(solution)/shard_map/all_to_all | solution.py:134
  63.4 1.4 collective-permute-done.7
  65.1 2.5 %all_gather.13 = bf16[128,10,258]{2,0,1:T(8,128)(2,1)S(1)} all-gather(bf16[64,10,258]{2,0,1:T(8,128)(2,1)S(1)} %maximum_select_fusion.1), channel_id=1, replica_groups=mesh['grp'=2,'lat'=4,'lon'=2,'ch'=2] {'ch'}, dimensions={0}, use_global_device_ids=true | all-gather | bytes 990720 | tf_op jit(solution)/shard_map/all_gather | solution.py:64
  67.6 1.2 fusion.152
  70.1 4.8 %all-to-all-start.2 = ((bf16[4,2,128,128]{3,2,1,0:T(8,128)(2,1)}), bf16[4,2,128,128]{3,2,1,0:T(8,128)(2,1)S(1)}, u32[]{:S(2)}, u32[]{:S(2)}) async-start(bf16[4,2,128,128]{3,2,1,0:T(8,128)(2,1)} %broadcast_select_fusion), calls=%async_computation.2 | async-start | bytes 524288 | tf_op jit(solution)/shard_map/all_to_all | solution.py:133
  74.9 18.2 %while.1 = (s32[]{:T(128)}, bf16[64,8,256]{2,0,1:T(8,128)(2,1)S(1)}, s32[8,3]{0,1:T(4,128)S(1)}, bf16[8,64,4,32]{1,3,2,0:T(8,128)(2,1)S(1)}, s32[]{:T(128)}) while((s32[]{:T(128)}, bf16[64,8,256]{2,0,1:T(8,128)(2,1)S(1)}, s32[8,3]{0,1:T(4,128)S(1)}, bf16[8,64,4,32]{1,3,2,0:T(8,128)(2,1)S(1)}, s32[]{:T(128)}) %tuple.87), condition=%wide.while_cond, body=%wide.while_body.sunk | while | flops 2 | bytes 163957 | solution.py:80
  75.6 1.4 constant_dynamic-slice_fusion.7
  77.8 1.4 constant_dynamic-slice_fusion.7
  80.1 1.4 constant_dynamic-slice_fusion.7
  82.4 1.4 constant_dynamic-slice_fusion.7
  84.6 1.4 constant_dynamic-slice_fusion.7
  86.9 1.4 constant_dynamic-slice_fusion.7
  89.2 1.4 constant_dynamic-slice_fusion.7
  91.5 1.4 constant_dynamic-slice_fusion.7
  93.1 1.0 fusion.164
  94.3 6.3 %scatter_custom_fusion.1 = f32[64,2048]{0,1:T(8,128)S(1)} fusion(s32[1024]{0:T(1024)S(1)} %reshape.338, f32[1024,64]{1,0:T(8,128)S(1)} %bitcast.128, f32[]{:T(128)} %constant.30.clone.1), kind=kCustom, calls=%fused_computation.104 | custom fusion | flops 65536 | bytes 524292
  101.0 2.1 %collective-permute-start.8 = (bf16[64,1,256]{2,0,1:T(8,128)(2,1)S(1)}, bf16[64,1,256]{2,0,1:T(8,128)(2,1)S(1)}, u32[]{:S(2)}, u32[]{:S(2)}) collective-permute-start(bf16[64,1,256]{2,0,1:T(8,128)(2,1)S(1)} %get-tuple-element.114), channel_id=1, source_target_pairs={{0,4},{4,8},{8,12},{12,0},{1,5},{5,9},{9,13},{13,1},{2,6},{6,10},{... | collective-permute-start | bytes 98312 | tf_op jit(solution)/shard_map/ppermute | solution.py:24
  103.1 2.0 %collective-permute-start.9 = (bf16[64,1,256]{2,0,1:T(8,128)(2,1)S(1)}, bf16[64,1,256]{2,0,1:T(8,128)(2,1)S(1)}, u32[]{:S(2)}, u32[]{:S(2)}) collective-permute-start(bf16[64,1,256]{2,0,1:T(8,128)(2,1)S(1)} %get-tuple-element.115), channel_id=1, source_target_pairs={{4,0},{8,4},{12,8},{0,12},{5,1},{9,5},{13,9},{1,13},{6,2},{10,6},{... | collective-permute-start | bytes 98312 | tf_op jit(solution)/shard_map/ppermute | solution.py:25
  105.1 1.6 %collective-permute-done.8 = bf16[64,1,256]{2,0,1:T(8,128)(2,1)S(1)} collective-permute-done((bf16[64,1,256]{2,0,1:T(8,128)(2,1)S(1)}, bf16[64,1,256]{2,0,1:T(8,128)(2,1)S(1)}, u32[]{:S(2)}, u32[]{:S(2)}) %collective-permute-start.8) | collective-permute-done | bytes 32800 | tf_op jit(solution)/shard_map/ppermute | solution.py:24
  107.3 1.6 %collective-permute-start.10 = (bf16[64,10,1]{2,0,1:T(8,128)(2,1)S(1)}, bf16[64,10,1]{2,0,1:T(8,128)(2,1)S(1)}, u32[]{:S(2)}, u32[]{:S(2)}) collective-permute-start(bf16[64,10,1]{2,0,1:T(8,128)(2,1)S(1)} %get-tuple-element.94), channel_id=1, source_target_pairs={{0,2},{2,0},{1,3},{3,1},{4,6},{6,4},{5,7},{7,5},{8,10},{10,8},{9,1... | collective-permute-start | bytes 3848 | tf_op jit(solution)/shard_map/ppermute | solution.py:24
  109.4 4.2 %collective-permute-done.10 = bf16[64,10,1]{2,0,1:T(8,128)(2,1)S(1)} collective-permute-done((bf16[64,10,1]{2,0,1:T(8,128)(2,1)S(1)}, bf16[64,10,1]{2,0,1:T(8,128)(2,1)S(1)}, u32[]{:S(2)}, u32[]{:S(2)}) %collective-permute-start.10) | collective-permute-done | bytes 1312 | tf_op jit(solution)/shard_map/ppermute | solution.py:24
  113.6 1.8 %collective-permute-done.11 = bf16[64,10,1]{2,0,1:T(8,128)(2,1)S(1)} collective-permute-done((bf16[64,10,1]{2,0,1:T(8,128)(2,1)S(1)}, bf16[64,10,1]{2,0,1:T(8,128)(2,1)S(1)}, u32[]{:S(2)}, u32[]{:S(2)}) %collective-permute-start.11) | collective-permute-done | bytes 1312 | tf_op jit(solution)/shard_map/ppermute | solution.py:25
  115.7 2.5 %all_gather.14 = bf16[128,10,258]{2,0,1:T(8,128)(2,1)S(1)} all-gather(bf16[64,10,258]{2,0,1:T(8,128)(2,1)S(1)} %maximum_select_fusion.2), channel_id=1, replica_groups=mesh['grp'=2,'lat'=4,'lon'=2,'ch'=2] {'ch'}, dimensions={0}, use_global_device_ids=true | all-gather | bytes 990720 | tf_op jit(solution)/shard_map/all_gather | solution.py:64
  118.2 1.2 fusion.151
  120.2 0.6 copy-done.10
  121.3 1.5 %collective-permute-start.12 = (bf16[64,1,256]{2,0,1:T(8,128)(2,1)S(1)}, bf16[64,1,256]{2,0,1:T(8,128)(2,1)S(1)}, u32[]{:S(2)}, u32[]{:S(2)}) collective-permute-start(bf16[64,1,256]{2,0,1:T(8,128)(2,1)S(1)} %get-tuple-element.112), channel_id=1, source_target_pairs={{0,4},{4,8},{8,12},{12,0},{1,5},{5,9},{9,13},{13,1},{2,6},{6,10},{... | collective-permute-start | bytes 98312 | tf_op jit(solution)/shard_map/ppermute | solution.py:24
  122.8 2.4 %collective-permute-start.13 = (bf16[64,1,256]{2,0,1:T(8,128)(2,1)S(1)}, bf16[64,1,256]{2,0,1:T(8,128)(2,1)S(1)}, u32[]{:S(2)}, u32[]{:S(2)}) collective-permute-start(bf16[64,1,256]{2,0,1:T(8,128)(2,1)S(1)} %get-tuple-element.113), channel_id=1, source_target_pairs={{4,0},{8,4},{12,8},{0,12},{5,1},{9,5},{13,9},{1,13},{6,2},{10,6},{... | collective-permute-start | bytes 98312 | tf_op jit(solution)/shard_map/ppermute | solution.py:25
  125.3 1.9 %collective-permute-done.12 = bf16[64,1,256]{2,0,1:T(8,128)(2,1)S(1)} collective-permute-done((bf16[64,1,256]{2,0,1:T(8,128)(2,1)S(1)}, bf16[64,1,256]{2,0,1:T(8,128)(2,1)S(1)}, u32[]{:S(2)}, u32[]{:S(2)}) %collective-permute-start.12) | collective-permute-done | bytes 32800 | tf_op jit(solution)/shard_map/ppermute | solution.py:24
  127.4 1.6 %collective-permute-start.14 = (bf16[64,10,1]{2,0,1:T(8,128)(2,1)S(1)}, bf16[64,10,1]{2,0,1:T(8,128)(2,1)S(1)}, u32[]{:S(2)}, u32[]{:S(2)}) collective-permute-start(bf16[64,10,1]{2,0,1:T(8,128)(2,1)S(1)} %get-tuple-element.92), channel_id=1, source_target_pairs={{0,2},{2,0},{1,3},{3,1},{4,6},{6,4},{5,7},{7,5},{8,10},{10,8},{9,1... | collective-permute-start | bytes 3848 | tf_op jit(solution)/shard_map/ppermute | solution.py:24
  129.5 5.0 %all-to-all-start.5 = ((bf16[4,2,64,128]{3,2,1,0:T(8,128)(2,1)}), bf16[4,2,64,128]{3,2,1,0:T(8,128)(2,1)S(1)}, u32[]{:S(2)}, u32[]{:S(2)}) async-start(bf16[4,2,64,128]{3,2,1,0:T(8,128)(2,1)} %bitcast.51), calls=%async_computation.5 | async-start | bytes 262144 | tf_op jit(solution)/shard_map/all_to_all | solution.py:148
  134.5 1.7 %collective-permute-done.15 = bf16[64,10,1]{2,0,1:T(8,128)(2,1)S(1)} collective-permute-done((bf16[64,10,1]{2,0,1:T(8,128)(2,1)S(1)}, bf16[64,10,1]{2,0,1:T(8,128)(2,1)S(1)}, u32[]{:S(2)}, u32[]{:S(2)}) %collective-permute-start.15) | collective-permute-done | bytes 1312 | tf_op jit(solution)/shard_map/ppermute | solution.py:25
  136.5 2.5 %all_gather.15 = bf16[128,10,258]{2,0,1:T(8,128)(2,1)S(1)} all-gather(bf16[64,10,258]{2,0,1:T(8,128)(2,1)S(1)} %maximum_select_fusion.3), channel_id=1, replica_groups=mesh['grp'=2,'lat'=4,'lon'=2,'ch'=2] {'ch'}, dimensions={0}, use_global_device_ids=true | all-gather | bytes 990720 | tf_op jit(solution)/shard_map/all_gather | solution.py:64
  139.1 1.2 fusion.150
  141.5 1.1 copy.160
  142.7 1.2 gather_fusion.5
  (160 shorter events, 20.7 us)
Async XLA Ops:
  0.6 17.0 %copy-start = (bf16[4,128,128]{2,1,0:T(8,128)(2,1)S(1)}, bf16[4,128,128]{2,1,0:T(8,128)(2,1)}, u32[]{:S(2)}) copy-start(bf16[4,128,128]{2,1,0:T(8,128)(2,1)} %param.14) | copy-start | bytes 393220
  0.6 14.6 %copy-start.3 = (bf16[3,3,128,128]{3,2,1,0:T(8,128)(2,1)S(1)}, bf16[3,3,128,128]{3,2,1,0:T(8,128)(2,1)}, u32[]{:S(2)}) copy-start(bf16[3,3,128,128]{3,2,1,0:T(8,128)(2,1)} %param.11) | copy-start | bytes 884740
  0.7 14.6 %copy-start.2 = (bf16[3,3,128,128]{3,2,1,0:T(8,128)(2,1)S(1)}, bf16[3,3,128,128]{3,2,1,0:T(8,128)(2,1)}, u32[]{:S(2)}) copy-start(bf16[3,3,128,128]{3,2,1,0:T(8,128)(2,1)} %param.13) | copy-start | bytes 884740
  1.9 34.5 %collective-permute-start = (bf16[64,1,256]{2,0,1:T(8,128)(2,1)S(1)}, bf16[64,1,256]{2,0,1:T(8,128)(2,1)S(1)}, u32[]{:S(2)}, u32[]{:S(2)}) collective-permute-start(bf16[64,1,256]{2,0,1:T(8,128)(2,1)S(1)} %copy.179), channel_id=1, source_target_pairs={{0,4},{4,8},{8,12},{12,0},{1,5},{5,9},{9,13},{13,1},{2,6},{6,10},{... | collective-permute-start | bytes 98312 | tf_op jit(solution)/shard_map/ppermute | solution.py:24
  5.0 31.5 %collective-permute-start.1 = (bf16[64,1,256]{2,0,1:T(8,128)(2,1)S(1)}, bf16[64,1,256]{2,0,1:T(8,128)(2,1)S(1)}, u32[]{:S(2)}, u32[]{:S(2)}) collective-permute-start(bf16[64,1,256]{2,0,1:T(8,128)(2,1)S(1)} %copy.180), channel_id=1, source_target_pairs={{4,0},{8,4},{12,8},{0,12},{5,1},{9,5},{13,9},{1,13},{6,2},{10,6},{... | collective-permute-start | bytes 98312 | tf_op jit(solution)/shard_map/ppermute | solution.py:25
  12.0 9.7 %all-to-all-start.1 = ((s32[4,1,2]{2,1,0:T(1,128)}), s32[4,1,2]{2,1,0:T(1,128)S(1)}, u32[]{:S(2)}, u32[]{:S(2)}) async-start(s32[4,1,2]{2,1,0:T(1,128)} %bitcast.13), calls=%async_computation.1 | async-start | bytes 4096 | tf_op jit(solution)/shard_map/all_to_all | solution.py:137
  15.3 0.7 copy-start.9
  15.3 1.0 copy-start.1
  15.7 2.6 %copy-start.6 = (bf16[4,64,128]{2,1,0:T(8,128)(2,1)S(1)}, bf16[4,64,128]{2,1,0:T(8,128)(2,1)}, u32[]{:S(2)}) copy-start(bf16[4,64,128]{2,1,0:T(8,128)(2,1)} %param.15) | copy-start | bytes 196612
  15.8 3.7 %copy-start.5 = (bf16[4,128]{1,0:T(4,128)(2,1)S(1)}, bf16[4,128]{1,0:T(4,128)(2,1)}, u32[]{:S(2)}) copy-start(bf16[4,128]{1,0:T(4,128)(2,1)} %param.16) | copy-start | bytes 3076
  17.0 19.3 %copy-start.8 = (s32[2]{0:T(128)S(1)}, s32[2]{0:T(128)}, u32[]{:S(2)}) copy-start(s32[2]{0:T(128)} %constant.64) | copy-start | bytes 28
  17.0 19.4 %copy-start.7 = (s32[2]{0:T(128)S(1)}, s32[2]{0:T(128)}, u32[]{:S(2)}) copy-start(s32[2]{0:T(128)} %constant.61) | copy-start | bytes 28
  17.6 18.8 %copy-start.4 = (bf16[64,8,256]{2,1,0:T(8,128)(2,1)S(1)}, bf16[64,8,256]{2,1,0:T(8,128)(2,1)}, u32[]{:S(2)}) copy-start(bf16[64,8,256]{2,1,0:T(8,128)(2,1)} %param.10) | copy-start | bytes 786436
  21.6 10.6 %all-to-all-start = ((s32[4,1,2]{2,1,0:T(1,128)}), s32[4,1,2]{2,1,0:T(1,128)S(1)}, u32[]{:S(2)}, u32[]{:S(2)}) async-start(s32[4,1,2]{2,1,0:T(1,128)} %bitcast.12), calls=%async_computation | async-start | bytes 4096 | tf_op jit(solution)/shard_map/all_to_all | solution.py:136
  32.2 26.4 %all-to-all-start.4 = ((bf16[4,2,128]{2,1,0:T(2,128)(2,1)}), bf16[4,2,128]{2,1,0:T(2,128)(2,1)S(1)}, u32[]{:S(2)}, u32[]{:S(2)}) async-start(bf16[4,2,128]{2,1,0:T(2,128)(2,1)} %broadcast_select_fusion.2), calls=%async_computation.4 | async-start | bytes 4096 | tf_op jit(solution)/shard_map/all_to_all | solution.py:135
  36.7 5.7 %collective-permute-start.2 = (bf16[64,10,1]{2,0,1:T(8,128)(2,1)S(1)}, bf16[64,10,1]{2,0,1:T(8,128)(2,1)S(1)}, u32[]{:S(2)}, u32[]{:S(2)}) collective-permute-start(bf16[64,10,1]{2,0,1:T(8,128)(2,1)S(1)} %get-tuple-element.98), channel_id=1, source_target_pairs={{0,2},{2,0},{1,3},{3,1},{4,6},{6,4},{5,7},{7,5},{8,10},{10,8},{9,1... | collective-permute-start | bytes 3848 | tf_op jit(solution)/shard_map/ppermute | solution.py:24
  38.3 5.8 %collective-permute-start.3 = (bf16[64,10,1]{2,0,1:T(8,128)(2,1)S(1)}, bf16[64,10,1]{2,0,1:T(8,128)(2,1)S(1)}, u32[]{:S(2)}, u32[]{:S(2)}) collective-permute-start(bf16[64,10,1]{2,0,1:T(8,128)(2,1)S(1)} %get-tuple-element.99), channel_id=1, source_target_pairs={{2,0},{0,2},{3,1},{1,3},{6,4},{4,6},{7,5},{5,7},{10,8},{8,10},{11,... | collective-permute-start | bytes 3848 | tf_op jit(solution)/shard_map/ppermute | solution.py:25
  50.2 5.8 %collective-permute-start.4 = (bf16[64,1,256]{2,0,1:T(8,128)(2,1)S(1)}, bf16[64,1,256]{2,0,1:T(8,128)(2,1)S(1)}, u32[]{:S(2)}, u32[]{:S(2)}) collective-permute-start(bf16[64,1,256]{2,0,1:T(8,128)(2,1)S(1)} %get-tuple-element.116), channel_id=1, source_target_pairs={{0,4},{4,8},{8,12},{12,0},{1,5},{5,9},{9,13},{13,1},{2,6},{6,10},{... | collective-permute-start | bytes 98312 | tf_op jit(solution)/shard_map/ppermute | solution.py:24
  51.9 4.3 %collective-permute-start.5 = (bf16[64,1,256]{2,0,1:T(8,128)(2,1)S(1)}, bf16[64,1,256]{2,0,1:T(8,128)(2,1)S(1)}, u32[]{:S(2)}, u32[]{:S(2)}) collective-permute-start(bf16[64,1,256]{2,0,1:T(8,128)(2,1)S(1)} %get-tuple-element.117), channel_id=1, source_target_pairs={{4,0},{8,4},{12,8},{0,12},{5,1},{9,5},{13,9},{1,13},{6,2},{10,6},{... | collective-permute-start | bytes 98312 | tf_op jit(solution)/shard_map/ppermute | solution.py:25
  56.4 7.1 %collective-permute-start.6 = (bf16[64,10,1]{2,0,1:T(8,128)(2,1)S(1)}, bf16[64,10,1]{2,0,1:T(8,128)(2,1)S(1)}, u32[]{:S(2)}, u32[]{:S(2)}) collective-permute-start(bf16[64,10,1]{2,0,1:T(8,128)(2,1)S(1)} %get-tuple-element.96), channel_id=1, source_target_pairs={{0,2},{2,0},{1,3},{3,1},{4,6},{6,4},{5,7},{7,5},{8,10},{10,8},{9,1... | collective-permute-start | bytes 3848 | tf_op jit(solution)/shard_map/ppermute | solution.py:24
  58.0 6.8 %collective-permute-start.7 = (bf16[64,10,1]{2,0,1:T(8,128)(2,1)S(1)}, bf16[64,10,1]{2,0,1:T(8,128)(2,1)S(1)}, u32[]{:S(2)}, u32[]{:S(2)}) collective-permute-start(bf16[64,10,1]{2,0,1:T(8,128)(2,1)S(1)} %get-tuple-element.97), channel_id=1, source_target_pairs={{2,0},{0,2},{3,1},{1,3},{6,4},{4,6},{7,5},{5,7},{10,8},{8,10},{11,... | collective-permute-start | bytes 3848 | tf_op jit(solution)/shard_map/ppermute | solution.py:25
  58.6 11.5 %all-to-all-start.3 = ((bf16[4,2,64,128]{3,2,1,0:T(8,128)(2,1)}), bf16[4,2,64,128]{3,2,1,0:T(8,128)(2,1)S(1)}, u32[]{:S(2)}, u32[]{:S(2)}) async-start(bf16[4,2,64,128]{3,2,1,0:T(8,128)(2,1)} %bitcast.17), calls=%async_computation.3 | async-start | bytes 262144 | tf_op jit(solution)/shard_map/all_to_all | solution.py:134
  70.1 23.0 %all-to-all-start.2 = ((bf16[4,2,128,128]{3,2,1,0:T(8,128)(2,1)}), bf16[4,2,128,128]{3,2,1,0:T(8,128)(2,1)S(1)}, u32[]{:S(2)}, u32[]{:S(2)}) async-start(bf16[4,2,128,128]{3,2,1,0:T(8,128)(2,1)} %broadcast_select_fusion), calls=%async_computation.2 | async-start | bytes 524288 | tf_op jit(solution)/shard_map/all_to_all | solution.py:133
  101.0 5.8 %collective-permute-start.8 = (bf16[64,1,256]{2,0,1:T(8,128)(2,1)S(1)}, bf16[64,1,256]{2,0,1:T(8,128)(2,1)S(1)}, u32[]{:S(2)}, u32[]{:S(2)}) collective-permute-start(bf16[64,1,256]{2,0,1:T(8,128)(2,1)S(1)} %get-tuple-element.114), channel_id=1, source_target_pairs={{0,4},{4,8},{8,12},{12,0},{1,5},{5,9},{9,13},{13,1},{2,6},{6,10},{... | collective-permute-start | bytes 98312 | tf_op jit(solution)/shard_map/ppermute | solution.py:24
  103.1 4.0 %collective-permute-start.9 = (bf16[64,1,256]{2,0,1:T(8,128)(2,1)S(1)}, bf16[64,1,256]{2,0,1:T(8,128)(2,1)S(1)}, u32[]{:S(2)}, u32[]{:S(2)}) collective-permute-start(bf16[64,1,256]{2,0,1:T(8,128)(2,1)S(1)} %get-tuple-element.115), channel_id=1, source_target_pairs={{4,0},{8,4},{12,8},{0,12},{5,1},{9,5},{13,9},{1,13},{6,2},{10,6},{... | collective-permute-start | bytes 98312 | tf_op jit(solution)/shard_map/ppermute | solution.py:25
  107.3 6.3 %collective-permute-start.10 = (bf16[64,10,1]{2,0,1:T(8,128)(2,1)S(1)}, bf16[64,10,1]{2,0,1:T(8,128)(2,1)S(1)}, u32[]{:S(2)}, u32[]{:S(2)}) collective-permute-start(bf16[64,10,1]{2,0,1:T(8,128)(2,1)S(1)} %get-tuple-element.94), channel_id=1, source_target_pairs={{0,2},{2,0},{1,3},{3,1},{4,6},{6,4},{5,7},{7,5},{8,10},{10,8},{9,1... | collective-permute-start | bytes 3848 | tf_op jit(solution)/shard_map/ppermute | solution.py:24
  108.9 6.4 %collective-permute-start.11 = (bf16[64,10,1]{2,0,1:T(8,128)(2,1)S(1)}, bf16[64,10,1]{2,0,1:T(8,128)(2,1)S(1)}, u32[]{:S(2)}, u32[]{:S(2)}) collective-permute-start(bf16[64,10,1]{2,0,1:T(8,128)(2,1)S(1)} %get-tuple-element.95), channel_id=1, source_target_pairs={{2,0},{0,2},{3,1},{1,3},{6,4},{4,6},{7,5},{5,7},{10,8},{8,10},{11,... | collective-permute-start | bytes 3848 | tf_op jit(solution)/shard_map/ppermute | solution.py:25
  119.8 1.0 copy-start.10
  121.3 5.8 %collective-permute-start.12 = (bf16[64,1,256]{2,0,1:T(8,128)(2,1)S(1)}, bf16[64,1,256]{2,0,1:T(8,128)(2,1)S(1)}, u32[]{:S(2)}, u32[]{:S(2)}) collective-permute-start(bf16[64,1,256]{2,0,1:T(8,128)(2,1)S(1)} %get-tuple-element.112), channel_id=1, source_target_pairs={{0,4},{4,8},{8,12},{12,0},{1,5},{5,9},{9,13},{13,1},{2,6},{6,10},{... | collective-permute-start | bytes 98312 | tf_op jit(solution)/shard_map/ppermute | solution.py:24
  122.8 4.4 %collective-permute-start.13 = (bf16[64,1,256]{2,0,1:T(8,128)(2,1)S(1)}, bf16[64,1,256]{2,0,1:T(8,128)(2,1)S(1)}, u32[]{:S(2)}, u32[]{:S(2)}) collective-permute-start(bf16[64,1,256]{2,0,1:T(8,128)(2,1)S(1)} %get-tuple-element.113), channel_id=1, source_target_pairs={{4,0},{8,4},{12,8},{0,12},{5,1},{9,5},{13,9},{1,13},{6,2},{10,6},{... | collective-permute-start | bytes 98312 | tf_op jit(solution)/shard_map/ppermute | solution.py:25
  127.4 7.1 %collective-permute-start.14 = (bf16[64,10,1]{2,0,1:T(8,128)(2,1)S(1)}, bf16[64,10,1]{2,0,1:T(8,128)(2,1)S(1)}, u32[]{:S(2)}, u32[]{:S(2)}) collective-permute-start(bf16[64,10,1]{2,0,1:T(8,128)(2,1)S(1)} %get-tuple-element.92), channel_id=1, source_target_pairs={{0,2},{2,0},{1,3},{3,1},{4,6},{6,4},{5,7},{7,5},{8,10},{10,8},{9,1... | collective-permute-start | bytes 3848 | tf_op jit(solution)/shard_map/ppermute | solution.py:24
  129.0 7.2 %collective-permute-start.15 = (bf16[64,10,1]{2,0,1:T(8,128)(2,1)S(1)}, bf16[64,10,1]{2,0,1:T(8,128)(2,1)S(1)}, u32[]{:S(2)}, u32[]{:S(2)}) collective-permute-start(bf16[64,10,1]{2,0,1:T(8,128)(2,1)S(1)} %get-tuple-element.93), channel_id=1, source_target_pairs={{2,0},{0,2},{3,1},{1,3},{6,4},{4,6},{7,5},{5,7},{10,8},{8,10},{11,... | collective-permute-start | bytes 3848 | tf_op jit(solution)/shard_map/ppermute | solution.py:25
  129.5 13.2 %all-to-all-start.5 = ((bf16[4,2,64,128]{3,2,1,0:T(8,128)(2,1)}), bf16[4,2,64,128]{3,2,1,0:T(8,128)(2,1)S(1)}, u32[]{:S(2)}, u32[]{:S(2)}) async-start(bf16[4,2,64,128]{3,2,1,0:T(8,128)(2,1)} %bitcast.51), calls=%async_computation.5 | async-start | bytes 262144 | tf_op jit(solution)/shard_map/all_to_all | solution.py:148
where the time goes:
time: 145 us; the launch traced here: 144 us
  starting transfers between devices  51.6 us (36%)
  local copies, waits for them, and re-layouts  35.9 us (25%)
  waiting for transfers between devices  24.5 us (17%)
  other arithmetic  13.2 us (9%)
  blocking collectives  10 us (7%)
  matrix products  7.13 us (5%)
    gather x48, local copies, waits for them, and re-layouts  17.9 us
    ppermute x8, starting transfers between devices, extended(): before = lax.ppermute(last, axis, up)  14.8 us
    ppermute x8, waiting for transfers between devices, extended(): before = lax.ppermute(last, axis, up)  13.1 us
    ppermute x8, starting transfers between devices, extended(): after = lax.ppermute(initial, axis, down)  10.6 us
    all_gather x4, blocking collectives, convolve(): lax.all_gather(padded, 'ch', axis=0, tiled=True)  10 us
    ppermute x8, waiting for transfers between devices, extended(): after = lax.ppermute(initial, axis, down)  7.17 us
    unnamed x5, other arithmetic  6.44 us
    dot_general x12, matrix products, apply_taps(): jnp.einsum('oi,ihw->ohw', row_kernel, stacked, preferred_element_type=jnp...  5.9 us
  transfers between devices with their start and end apart: 22, of which 13 were waited for; matrix products, arithmetic and copies ran while one was open for 28% of the time, Pallas kernels for 0%

commit v1 on v0

v1 whole, which is shorter than its diff:
```python
import functools

import jax
import jax.numpy as jnp
from jax import lax
from jax.experimental import pallas as pl
from jax.experimental.pallas import tpu as pltpu
from jax.sharding import PartitionSpec as P

PH = 4
PW = 32
CAP = 2
HALO = 2
SIDE = 16
META = 16

keep_rate = 0.6
blend_rate = 0.4
guide_rate = 0.3

MESH = pl.DeviceIdType.MESH
F32 = jnp.float32
BF16 = jnp.bfloat16


def kernel(
    n_lat, n_lon, rows, width, half, blocks,
    dest, row_off, col_off, x, kfi, kfo, kao, kai, bias, weight, values, scale,
    out, inn_out,
    both, X, X3, pre, base, D, E, pay, R, G, GF, inn, inn_r, out_s, out_r, pulled_s,
    plan,
    halo_s, halo_r, pair_s, pair_r, pay_s, pay_r, inn_ss, inn_rs,
):
    lat, lon, ch = lax.axis_index("lat"), lax.axis_index("lon"), lax.axis_index("ch")
    other = 1 - ch
    chans = 2 * half
    obs = weight.shape[1]
    cells = PH * PW
    pitch = width + 2 * SIDE
    slots = n_lat * CAP
    px = rows * width
    lon_right = lax.rem(lon + ch, n_lon)
    lon_left = lax.rem(lon + n_lon - other, n_lon)
    has_up = lat > 0
    has_down = lat < n_lat - 1
    sibling = {"ch": other}

    def at(dlat, side):
        place = {"lat": lat + dlat}
        if side:
            place["lon"] = lon_right if side > 0 else lon_left
            place["ch"] = other
        return place

    barrier = pltpu.get_barrier_semaphore()

    def greet(place):
        pl.semaphore_signal(barrier, inc=1, device_id=place, device_id_type=MESH)

    for step in range(1, n_lat):
        greet({"lat": lax.rem(lat + step, n_lat)})
    greet(at(0, -1))
    greet(at(0, 1))

    @pl.when(has_up)
    def _():
        greet(at(-1, -1))
        greet(at(-1, 1))

    @pl.when(has_down)
    def _():
        greet(at(1, -1))
        greet(at(1, 1))

    def count_block(b, _):
        def earlier(e, rank):
            return rank + jnp.where(dest[e] == dest[b], 1, 0)

        plan[b] = dest[b] * CAP + lax.fori_loop(0, b, earlier, 0)
        return 0

    for b in range(blocks) if blocks <= 8 else ():
        rank = 0
        for e in range(b):
            rank = rank + jnp.where(dest[e] == dest[b], 1, 0)
        plan[b] = dest[b] * CAP + rank
    if blocks > 8:
        lax.fori_loop(0, blocks, count_block, 0)

    def pack_slot(s, _):
        def look(b, found):
            return jnp.where(plan[b] == s, b, found)

        found = lax.fori_loop(0, blocks, look, -1)
        source = jnp.maximum(found, 0)
        fill = jnp.where(found >= 0, 1.0, 0.0)
        w = (weight[source].astype(F32) * fill).astype(BF16)
        t = s // CAP
        k = s % CAP
        pay[t, k, 0:half] = w_half(w)
        pay[t, k, half:chans] = values[source]
        level = lax.broadcasted_iota(jnp.int32, (META, obs), 0)
        r0 = row_off[source].astype(F32)
        q0 = col_off[source].astype(F32)
        meta = jnp.where(level == 0, scale[source], jnp.where(level == 1, r0, q0))
        pay[t, k, chans : chans + META] = meta.astype(BF16)
        return 0

    def w_half(w):
        return jnp.where(ch == 0, w[0:half].astype(F32), w[half:chans].astype(F32)).astype(BF16)

    lax.fori_loop(0, slots, pack_slot, 0)

    tops = (lat + n_lat - 1) // n_lat
    bottoms = (2 * n_lat - 2 - lat) // n_lat
    pl.semaphore_wait(barrier, n_lat + 1 + 2 * tops + 2 * bottoms)

    def pair_copy(src, dst, i):
        return pltpu.make_async_remote_copy(
            src_ref=src, dst_ref=dst, send_sem=pair_s.at[i], recv_sem=pair_r.at[i],
            device_id=sibling, device_id_type=MESH,
        )

    reshard = pair_copy(x.at[other], both.at[ch], 0)
    reshard.start()
    both[ch] = x[ch]

    top, left = HALO, SIDE
    spans_r = {-1: (top, 0 + rows + top), 0: (top, top), 1: (top + rows - HALO, 0)}
    spans_c = {-1: (left, left + width), 0: (left, left), 1: (left + width - SIDE, 0)}
    size_r = {-1: HALO, 0: rows, 1: HALO}
    size_c = {-1: SIDE, 0: width, 1: SIDE}
    routes = [(0, -1), (0, 1), (-1, 0), (-1, -1), (-1, 1), (1, 0), (1, -1), (1, 1)]

    def halo_copy(buf, i, base_sem):
        dl, side = routes[i]
        sr, dr = spans_r[dl]
        sc, dc = spans_c[side]
        src = buf.at[pl.ds(sr, size_r[dl]), pl.ds(sc, size_c[side])]
        dst = buf.at[pl.ds(dr, size_r[dl]), pl.ds(dc, size_c[side])]
        return pltpu.make_async_remote_copy(
            src_ref=src, dst_ref=dst,
            send_sem=halo_s.at[base_sem + i], recv_sem=halo_r.at[base_sem + i],
            device_id=at(dl, side), device_id_type=MESH,
        )

    def halo_wait_recv(buf, i, base_sem):
        halo_copy(buf, i, base_sem).wait_recv()

    def guarded(dl, fn):
        if dl == 0:
            fn()
        else:
            pl.when(has_up if dl < 0 else has_down)(fn)

    def halo_start(buf, base_sem):
        for dl in (-1, 1, 0):
            def go(dl=dl):
                for i, route in enumerate(routes):
                    if route[0] == dl:
                        halo_copy(buf, i, base_sem).start()

            guarded(dl, go)

    def halo_finish(buf, base_sem):
        for dl in (0, -1, 1):
            def go(dl=dl):
                for i, route in enumerate(routes):
                    if route[0] == dl:
                        halo_copy(buf, i, base_sem).wait_send()

            def got(dl=dl):
                for i, route in enumerate(routes):
                    if route[0] == dl:
                        halo_wait_recv(buf, i, base_sem)

            guarded(dl, go)
            guarded(-dl, got)

    def clear_poles(buf):
        @pl.when(lat == 0)
        def _():
            buf[0:HALO] = jnp.zeros((HALO, pitch, chans), BF16)

        @pl.when(lat == n_lat - 1)
        def _():
            buf[rows + HALO : rows + 2 * HALO] = jnp.zeros((HALO, pitch, chans), BF16)

    def put_row(r, v):
        X3[r * pitch : (r + 1) * pitch, 0:chans] = pltpu.roll(v, 1, 0).astype(BF16)
        X3[r * pitch : (r + 1) * pitch, chans : 2 * chans] = v.astype(BF16)
        X3[r * pitch : (r + 1) * pitch, 2 * chans :] = pltpu.roll(v, pitch - 1, 0).astype(BF16)

    def conv(kmat, first, count):
        acc = None
        for a in range(3):
            part = jnp.dot(
                X3[(first + a) * pitch : (first + a + count) * pitch, :], kmat[a],
                preferred_element_type=F32,
            )
            acc = part if acc is None else acc + part
        return acc

    def edge_factor(r):
        if r == 0:
            return jnp.where(has_up, 1.0, 0.0)
        if r == rows + 1:
            return jnp.where(has_down, 1.0, 0.0)
        return None

    clear_poles(X)
    clear_poles(G)

    reshard.wait()
    for r in range(rows):
        X[top + r, left : left + width] = jnp.concatenate([both[0, r], both[1, r]], axis=-1)
    halo_start(X, 0)

    def pay_copy(i, step):
        peer = lax.rem(lat + step, n_lat)
        return pltpu.make_async_remote_copy(
            src_ref=pay.at[peer], dst_ref=R.at[lat, ch],
            send_sem=pay_s.at[i], recv_sem=pay_r.at[i],
            device_id={"lat": peer}, device_id_type=MESH,
        )

    for step in range(1, n_lat):
        pay_copy(step - 1, step).start()
    R[lat, ch] = pay[lat]

    halo_finish(X, 0)
    for r in range(rows + 2 * HALO):
        put_row(r, X[r].astype(F32))

    CH = 2
    for r0 in range(0, rows + 2, CH):
        acc = conv(kfi, r0, CH) + bias[...]
        pre[r0 * pitch : (r0 + CH) * pitch, :] = acc
    for r in range(rows + 2):
        v = pre[r * pitch : (r + 1) * pitch, :]
        h = v / (1.0 + jnp.exp(-v))
        f = edge_factor(r)
        if f is not None:
            h = h * f
        put_row(r, h.astype(BF16).astype(F32))

    for step in range(1, n_lat):
        pay_copy(step - 1, step).wait()
    forward = pair_copy(R.at[:, ch], R.at[:, ch], 1)
    forward.start()

    for r0 in range(0, rows, CH):
        acc = conv(kfo, r0, CH)
        for i in range(CH):
            r = r0 + i
            state = X[top + r, left : left + width].astype(F32)
            den = (state + acc[i * pitch + left : i * pitch + left + width]).astype(BF16)
            base[r * width : (r + 1) * width, :] = keep_rate * state + blend_rate * den.astype(F32)
            D[ch, :, r * width : (r + 1) * width] = den.astype(F32).T.astype(BF16)
    swap = pair_copy(D.at[ch], D.at[ch], 2)
    swap.start()

    forward.wait()
    lane = lax.broadcasted_iota(jnp.int32, (1, cells), 1)
    cell_r = (lane // PW).astype(F32)
    cell_c = (lane % PW).astype(F32)

    def place_slot(s, _):
        t = s // CAP
        k = s % CAP
        meta = R[t, 0, k, chans : chans + META].astype(F32)
        q = meta[2:3] + cell_c
        target = (meta[1:2] + cell_r) * width + q + jnp.where(q >= width, float(px - width), 0.0)
        index = lax.broadcasted_iota(jnp.int32, (2 * px, cells), 0).astype(F32)
        E[s] = jnp.where(index == target, 1.0, 0.0).astype(BF16)
        return 0

    lax.fori_loop(0, slots, place_slot, 0)
    swap.wait()

    def observe_slot(s, _):
        t = s // CAP
        k = s % CAP
        patch = jnp.dot(D[0], E[s, 0:px], preferred_element_type=F32) + jnp.dot(
            D[1], E[s, px : 2 * px], preferred_element_type=F32
        )
        w = jnp.concatenate([R[t, 0, k, 0:half], R[t, 1, k, 0:half]], axis=0)
        val = jnp.concatenate([R[t, 0, k, half:chans], R[t, 1, k, half:chans]], axis=0)
        predicted = lax.dot_general(
            patch.astype(BF16), w, (((1,), (1,)), ((), ())), preferred_element_type=F32
        )
        residual = predicted - val.astype(F32)
        inn[t, k] = jnp.where(ch == 0, residual[0:half], residual[half:chans]).astype(BF16)
        sc = R[t, 0, k, chans : chans + META].astype(F32)[0:1]
        weighted = (residual * sc).astype(BF16)
        pulled_s[s] = jnp.dot(weighted, w, preferred_element_type=F32).astype(BF16)
        return 0

    lax.fori_loop(0, slots, observe_slot, 0)

    GF[...] = jnp.zeros((px, chans), F32)

    def spread_slot(s, _):
        GF[...] += lax.dot_general(
            E[s, pl.ds(pl.multiple_of(ch * px, px), px)], pulled_s[s],
            (((1,), (1,)), ((), ())), preferred_element_type=F32,
        )
        return 0

    lax.fori_loop(0, slots, spread_slot, 0)
    for r in range(rows):
        G[top + r, left : left + width] = GF[r * width : (r + 1) * width, :].astype(BF16)
    halo_start(G, 8)

    def inn_copy(i, step):
        peer = lax.rem(lat + step, n_lat)
        return pltpu.make_async_remote_copy(
            src_ref=inn.at[peer], dst_ref=inn_r.at[lat],
            send_sem=inn_ss.at[i], recv_sem=inn_rs.at[i],
            device_id={"lat": peer}, device_id_type=MESH,
        )

    for step in range(1, n_lat):
        inn_copy(step - 1, step).start()
    inn_r[lat] = inn[lat]
    halo_finish(G, 8)
    for r in range(rows + 2 * HALO):
        put_row(r, G[r].astype(F32))
    for r0 in range(0, rows + 2, CH):
        part = slice(r0 * pitch, (r0 + CH) * pitch)
        back = conv(kao, r0, CH)
        v = pre[part, :]
        s = 1.0 / (1.0 + jnp.exp(-v))
        pre[part, :] = back * s * (1.0 + v * (1.0 - s))
    for r in range(rows + 2):
        g = pre[r * pitch : (r + 1) * pitch, :]
        f = edge_factor(r)
        if f is not None:
            g = g * f
        put_row(r, g.astype(BF16).astype(F32))
    for r0 in range(0, rows, CH):
        acc = conv(kai, r0, CH)
        for i in range(CH):
            r = r0 + i
            own = slice(r * width, (r + 1) * width)
            grad = GF[own, :] + acc[i * pitch + left : i * pitch + left + width]
            res = (base[own, :] - guide_rate * grad).T
            out_s[0, :, own] = res[0:half]
            out_s[1, :, own] = res[half:chans]
    back_home = pair_copy(out_s.at[other], out_r, 3)
    back_home.start()
    out[ch] = out_s[ch]
    for step in range(1, n_lat):
        inn_copy(step - 1, step).wait()

    def fetch(b, _):
        slot = plan[b]
        inn_out[b] = inn_r[slot // CAP, slot % CAP]
        return 0

    lax.fori_loop(0, blocks, fetch, 0)
    back_home.wait()
    out[other] = out_r[...]


def body(n_lat, n_lon, noisy_state, kernel_in, bias_in, kernel_out, interp_weight, observed,
         obs_precision, dest_tile, row_offset, col_offset):
    half, rows, cols = noisy_state.shape
    chans = 2 * half
    width = cols // 2
    blocks, obs, cells = interp_weight.shape
    slots = n_lat * CAP
    pitch = width + 2 * SIDE
    px = rows * width
    x = jnp.transpose(noisy_state.reshape(half, rows, 2, width), (2, 1, 3, 0))

    def forward(k):
        return jnp.transpose(k, (0, 1, 3, 2)).reshape(3, 3 * chans, chans)

    def adjoint(k):
        return k[::-1, ::-1].reshape(3, 3 * chans, chans)

    vmem = pl.BlockSpec(memory_space=pltpu.VMEM)
    smem = pl.BlockSpec(memory_space=pltpu.SMEM)
    call = pl.pallas_call(
        functools.partial(kernel, n_lat, n_lon, rows, width, half, blocks),
        out_shape=(
            jax.ShapeDtypeStruct((2, half, px), F32),
            jax.ShapeDtypeStruct((blocks, half, obs), BF16),
        ),
        in_specs=[smem] * 3 + [vmem] * 9,
        out_specs=(vmem, vmem),
        scratch_shapes=[
            pltpu.VMEM((2, rows, width, half), BF16),
            pltpu.VMEM((rows + 4, pitch, chans), BF16),
            pltpu.VMEM(((rows + 4) * pitch, 3 * chans), BF16),
            pltpu.VMEM(((rows + 2) * pitch, chans), F32),
            pltpu.VMEM((px, chans), F32),
            pltpu.VMEM((2, chans, px), BF16),
            pltpu.VMEM((slots, 2 * px, cells), BF16),
            pltpu.VMEM((n_lat, CAP, chans + META, obs), BF16),
            pltpu.VMEM((n_lat, 2, CAP, chans + META, obs), BF16),
            pltpu.VMEM((rows + 4, pitch, chans), BF16),
            pltpu.VMEM((px, chans), F32),
            pltpu.VMEM((n_lat, CAP, half, obs), BF16),
            pltpu.VMEM((n_lat, CAP, half, obs), BF16),
            pltpu.VMEM((2, half, px), F32),
            pltpu.VMEM((half, px), F32),
            pltpu.VMEM((slots, chans, cells), BF16),
            pltpu.SMEM((blocks,), jnp.int32),
            pltpu.SemaphoreType.DMA((16,)),
            pltpu.SemaphoreType.DMA((16,)),
            pltpu.SemaphoreType.DMA((4,)),
            pltpu.SemaphoreType.DMA((4,)),
            pltpu.SemaphoreType.DMA((n_lat - 1,)),
            pltpu.SemaphoreType.DMA((n_lat - 1,)),
            pltpu.SemaphoreType.DMA((n_lat - 1,)),
            pltpu.SemaphoreType.DMA((n_lat - 1,)),
        ],
        compiler_params=pltpu.CompilerParams(
            collective_id=0, has_side_effects=True, vmem_limit_bytes=63 * 1024 * 1024
        ),
    )
    out, innovation = call(
        dest_tile, row_offset, col_offset, x,
        forward(kernel_in), forward(kernel_out), adjoint(kernel_out), adjoint(kernel_in),
        bias_in.reshape(1, chans), interp_weight, observed,
        obs_precision.astype(F32).reshape(blocks, 1, obs),
    )
    next_state = jnp.transpose(out.reshape(2, half, rows, width), (1, 2, 0, 3))
    return next_state.reshape(half, rows, cols), innovation


def solution(mesh):
    return jax.shard_map(
        functools.partial(body, mesh.shape["lat"], mesh.shape["lon"]),
        mesh=mesh,
        in_specs=(
            P(("grp", "ch"), "lat", "lon"),
            P(),
            P(),
            P(),
            P(("grp", "lat", "lon"), None, None),
            P(("grp", "lat", "lon"), "ch", None),
            P(("grp", "lat", "lon"), None),
            P(("grp", "lat", "lon")),
            P(("grp", "lat", "lon")),
            P(("grp", "lat", "lon")),
        ),
        out_specs=(P(("grp", "ch"), "lat", "lon"), P(("grp", "lat", "lon"), "ch", None)),
        check_vma=False,
    )
```

time: 145 us -> 46.7 us (0.32)
  starting transfers between devices: 51.6 us -> 0 us
  Pallas kernels: 0 us -> 35.9 us
  local copies, waits for them, and re-layouts: 35.9 us -> 9.24 us
  waiting for transfers between devices: 24.5 us -> 0 us
  other arithmetic: 13.2 us -> 0.58 us
  blocking collectives: 10 us -> 0 us
  matrix products: 7.13 us -> 0 us
    pallas_call x0 -> x1, Pallas kernels: none -> 35.9 us  [body(): call(dest_tile, row_offset, col_offset, x, forward(kernel_in), forward(ke...]
    all_to_all x6 -> x0, starting transfers between devices: 26.2 us -> none  [the longest x1 5.06 us: observe(): lax.all_to_all(rows_out, 'lat', split_axis=0, concat_axis=0, tiled=True)]
    ppermute x16 -> x0, starting transfers between devices: 25.4 us -> none  [the longest x8 14.8 us: extended(): before = lax.ppermute(last, axis, up)]
    gather x54 -> x0, local copies, waits for them, and re-layouts: 23.4 us -> none
    ppermute x16 -> x0, waiting for transfers between devices: 20.3 us -> none  [the longest x8 13.1 us: extended(): before = lax.ppermute(last, axis, up)]
    all_gather x4 -> x0, blocking collectives: 10 us -> none  [convolve(): lax.all_gather(padded, 'ch', axis=0, tiled=True)]
    dot_general x14 -> x0, matrix products: 7.13 us -> none  [the longest x12 5.9 us: apply_taps(): jnp.einsum('oi,ihw->ohw', row_kernel, stacked, preferred_element_type=jnp...]
    unnamed x5 -> x0, other arithmetic: 6.44 us -> none
  transfers between devices with their start and end apart: 22 -> 0, of which waited for: 13 -> 0; matrix products, arithmetic and copies ran while one was open for 28% -> 0% of each run, Pallas kernels for 0% -> 0%
where the time goes in v1:
time: 46.7 us; the launch traced here: 46.4 us
  Pallas kernels  35.9 us (77%)
  local copies, waits for them, and re-layouts  9.24 us (20%)
  between operations  0.66 us (1%)
  other arithmetic  0.58 us (1%)
    pallas_call x1, Pallas kernels, body(): call(dest_tile, row_offset, col_offset, x, forward(kernel_in), forward(ke...  35.9 us
    unnamed x12, local copies, waits for them, and re-layouts  3.08 us
    transpose x2, local copies, waits for them, and re-layouts, forward(): return jnp.transpose(k, (0, 1, 3, 2)).reshape(3, 3 * chans, chans)  2.77 us
    rev x2, local copies, waits for them, and re-layouts, adjoint(): return k[::-1, ::-1].reshape(3, 3 * chans, chans)  1.48 us
    reshape x1, local copies, waits for them, and re-layouts, body(): x = jnp.transpose(noisy_state.reshape(half, rows, 2, width), (2, 1, 3, 0))  1.07 us

profile of v1, /device:TPU:0, one launch (start us, length us, event | category | flops | bytes accessed | tf_op | source)
XLA Modules:
  0.0 46.4 jit_solution(15571608593441734280)
XLA Ops:
  0.6 0.0 copy-start.4
  0.6 0.7 %copy-done.4 = bf16[4,128]{1,0:T(4,128)(2,1)S(1)} copy-done((bf16[4,128]{1,0:T(4,128)(2,1)S(1)}, bf16[4,128]{1,0:T(4,128)(2,1)}, u32[]{:S(2)}) %copy-start.4) | copy-done | bytes 1048
  1.3 0.6 %reshape.43 = f32[4,128]{1,0:T(4,128)} convert(bf16[4,128]{1,0:T(4,128)(2,1)S(1)} %copy-done.4) | non-fusion elementwise | flops 512 | bytes 3072 | tf_op jit(solution)/shard_map/reshape | solution.py:428
  1.9 0.0 copy-start
  1.9 1.9 %copy.17 = bf16[3,3,128,128]{3,2,1,0:T(8,128)(2,1)} copy(bf16[3,3,128,128]{2,3,1,0:T(8,128)(2,1)} %bitcast.26) | data formatting | bytes 589824 | tf_op jit(solution)/shard_map/transpose | solution.py:378
  3.8 0.0 copy-done
  3.8 0.9 %copy.16 = bf16[3,3,128,128]{3,2,1,0:T(8,128)(2,1)} copy(bf16[3,3,128,128]{2,3,1,0:T(8,128)(2,1)S(1)} %bitcast.25) | data formatting | bytes 589824 | tf_op jit(solution)/shard_map/transpose | solution.py:378
  4.7 0.0 copy-start.1
  4.7 0.7 %rev.7 = bf16[3,3,128,128]{3,2,1,0:T(8,128)(2,1)} reverse(bf16[3,3,128,128]{3,2,1,0:T(8,128)(2,1)S(1)} %copy-done), dimensions={0,1} | reverse | bytes 589824 | tf_op jit(solution)/shard_map/rev | solution.py:381
  5.4 0.3 copy-done.1
  5.7 0.0 copy-start.2
  5.7 0.7 %rev.6 = bf16[3,3,128,128]{3,2,1,0:T(8,128)(2,1)} reverse(bf16[3,3,128,128]{3,2,1,0:T(8,128)(2,1)S(1)} %copy-done.1), dimensions={0,1} | reverse | bytes 589824 | tf_op jit(solution)/shard_map/rev | solution.py:381
  6.5 0.3 copy-done.2
  6.8 1.1 %copy.15 = bf16[64,8,2,128]{0,3,1,2:T(8,128)(2,1)} copy(bf16[64,8,2,128]{3,1,2,0:T(8,128)(2,1)S(1)} %bitcast.32) | data formatting | bytes 524288 | tf_op jit(solution)/shard_map/reshape | solution.py:375
  7.9 35.9 %shard_map.113 = (f32[2,64,1024]{2,1,0:T(8,128)}, bf16[4,64,128]{2,1,0:T(8,128)(2,1)}) custom-call(s32[4]{0:T(128)} %dest.1, s32[4]{0:T(128)} %row_off.1, s32[4]{0:T(128)} %col_off.1, bf16[2,8,128,64]{3,2,1,0:T(8,128)(2,1)} %bitcast.24, bf16[3,384,128]{2,1,0:T(8,128)(2,1)} %bitcast.28, bf16[3,384,128]{2,1,0:T(8,128)(2,1)} %bitcast.27, ...), custom_call_target="tpu_custom_call" | custom-call | tf_op jit(solution)/shard_map/pallas_call | solution.py:424
  43.8 1.1 %copy.19 = f32[16,8,8,128]{3,2,1,0:T(8,128)S(1)} copy(f32[16,8,8,128]{3,1,2,0:T(8,128)} %bitcast.31) | data formatting | bytes 1048576
  44.9 0.0 copy-start.3
  44.9 0.8 %copy_bitcast_fusion = f32[64,8,256]{2,1,0:T(8,128)} fusion(f32[2,64,8,128]{3,2,1,0:T(8,128)S(1)} %bitcast.23), kind=kLoop, calls=%fused_computation.1 | loop fusion | bytes 1048576 | tf_op jit(solution)/shard_map/reshape | solution.py:431
  45.8 0.0 copy-done.3
  45.8 0.6 %copy.22 = bf16[4,64,128]{2,1,0:T(8,128)(2,1)} copy(bf16[4,64,128]{2,1,0:T(8,128)(2,1)S(1)} %copy-done.3) | data formatting | bytes 131072
Async XLA Ops:
  0.6 0.7 %copy-start.4 = (bf16[4,128]{1,0:T(4,128)(2,1)S(1)}, bf16[4,128]{1,0:T(4,128)(2,1)}, u32[]{:S(2)}) copy-start(bf16[4,128]{1,0:T(4,128)(2,1)} %param.16) | copy-start | bytes 3076
  1.9 1.9 %copy-start = (bf16[3,3,128,128]{3,2,1,0:T(8,128)(2,1)S(1)}, bf16[3,3,128,128]{3,2,1,0:T(8,128)(2,1)}, u32[]{:S(2)}) copy-start(bf16[3,3,128,128]{3,2,1,0:T(8,128)(2,1)} %param.11) | copy-start | bytes 884740
  4.7 1.1 %copy-start.1 = (bf16[3,3,128,128]{3,2,1,0:T(8,128)(2,1)S(1)}, bf16[3,3,128,128]{3,2,1,0:T(8,128)(2,1)}, u32[]{:S(2)}) copy-start(bf16[3,3,128,128]{3,2,1,0:T(8,128)(2,1)} %param.13) | copy-start | bytes 884740
  5.7 1.0 %copy-start.2 = (bf16[64,8,256]{2,1,0:T(8,128)(2,1)S(1)}, bf16[64,8,256]{2,1,0:T(8,128)(2,1)}, u32[]{:S(2)}) copy-start(bf16[64,8,256]{2,1,0:T(8,128)(2,1)} %param.10) | copy-start | bytes 786436
  44.9 0.8 %copy-start.3 = (bf16[4,64,128]{2,1,0:T(8,128)(2,1)S(1)}, bf16[4,64,128]{2,1,0:T(8,128)(2,1)}, u32[]{:S(2)}) copy-start(bf16[4,64,128]{2,1,0:T(8,128)(2,1)} %get-tuple-element.9) | copy-start | bytes 196612

commit v2 on v1

--- a/solution.py
+++ b/solution.py
@@ -13,6 +13,7 @@
 HALO = 2
 SIDE = 16
 META = 16
+GROUP = 8
 
 keep_rate = 0.6
 blend_rate = 0.4
@@ -25,8 +26,9 @@
 
 def kernel(
     n_lat, n_lon, rows, width, half, blocks,
-    dest, row_off, col_off, x, kfi, kfo, kao, kai, bias, weight, values, scale,
+    dest, row_off, col_off, x_hbm, kin_hbm, kout_hbm, bias, weight_hbm, values_hbm, scale_hbm,
     out, inn_out,
+    xv, xs, x_send, kin, kout, weight, values, scale_raw, scale, kfi, kfo, load_sem,
     both, X, X3, pre, base, D, E, pay, R, G, GF, inn, inn_r, out_s, out_r, pulled_s,
     plan,
     halo_s, halo_r, pair_s, pair_r, pay_s, pay_r, inn_ss, inn_rs,
@@ -34,7 +36,7 @@
     lat, lon, ch = lax.axis_index("lat"), lax.axis_index("lon"), lax.axis_index("ch")
     other = 1 - ch
     chans = 2 * half
-    obs = weight.shape[1]
+    obs = weight_hbm.shape[1]
     cells = PH * PW
     pitch = width + 2 * SIDE
     slots = n_lat * CAP
@@ -52,6 +54,15 @@
             place["ch"] = other
         return place
 
+    loads = [
+        pltpu.make_async_copy(src, dst, load_sem.at[i])
+        for i, (src, dst) in enumerate(
+            [(x_hbm, xv), (weight_hbm, weight), (values_hbm, values), (scale_hbm, scale_raw),
+             (kin_hbm, kin), (kout_hbm, kout)]
+        )
+    ]
+    for load in loads:
+        load.start()
     barrier = pltpu.get_barrier_semaphore()
 
     def greet(place):
@@ -102,14 +113,20 @@
         level = lax.broadcasted_iota(jnp.int32, (META, obs), 0)
         r0 = row_off[source].astype(F32)
         q0 = col_off[source].astype(F32)
-        meta = jnp.where(level == 0, scale[source], jnp.where(level == 1, r0, q0))
+        meta = jnp.where(level == 0, scale[pl.ds(source, 1), :], jnp.where(level == 1, r0, q0))
         pay[t, k, chans : chans + META] = meta.astype(BF16)
         return 0
 
     def w_half(w):
         return jnp.where(ch == 0, w[0:half].astype(F32), w[half:chans].astype(F32)).astype(BF16)
 
-    lax.fori_loop(0, slots, pack_slot, 0)
+    loads[0].wait()
+    for h in range(2):
+        part = xv[:, :, h * width : (h + 1) * width].astype(F32)
+        xs[h] = part.reshape(half * rows, width)
+    for r in range(rows):
+        both[ch, r] = xs[ch, pl.ds(r, half, stride=rows), :].astype(BF16)
+        x_send[r] = xs[other, pl.ds(r, half, stride=rows), :].astype(BF16)
 
     tops = (lat + n_lat - 1) // n_lat
     bottoms = (2 * n_lat - 2 - lat) // n_lat
@@ -121,9 +138,12 @@
             device_id=sibling, device_id_type=MESH,
         )
 
-    reshard = pair_copy(x.at[other], both.at[ch], 0)
+    reshard = pair_copy(x_send, both.at[ch], 0)
     reshard.start()
-    both[ch] = x[ch]
+    for load in loads[1:4]:
+        load.wait()
+    scale[...] = scale_raw[...].astype(F32)
+    lax.fori_loop(0, slots, pack_slot, 0)
 
     top, left = HALO, SIDE
     spans_r = {-1: (top, 0 + rows + top), 0: (top, top), 1: (top + rows - HALO, 0)}
@@ -195,11 +215,14 @@
         acc = None
         for a in range(3):
             part = jnp.dot(
-                X3[(first + a) * pitch : (first + a + count) * pitch, :], kmat[a],
+                X3[(first + a) * pitch : (first + a + count) * pitch, :], kmat(a),
                 preferred_element_type=F32,
             )
             acc = part if acc is None else acc + part
         return acc
+
+    def mirrored(k, a):
+        return jnp.concatenate([k[2 - a, 2], k[2 - a, 1], k[2 - a, 0]], axis=0)
 
     def edge_factor(r):
         if r == 0:
@@ -213,7 +236,9 @@
 
     reshard.wait()
     for r in range(rows):
-        X[top + r, left : left + width] = jnp.concatenate([both[0, r], both[1, r]], axis=-1)
+        X[top + r, left : left + width] = (
+            jnp.concatenate([both[0, r], both[1, r]], axis=0).astype(F32).T.astype(BF16)
+        )
     halo_start(X, 0)
 
     def pay_copy(i, step):
@@ -227,6 +252,12 @@
     for step in range(1, n_lat):
         pay_copy(step - 1, step).start()
     R[lat, ch] = pay[lat]
+    for load in loads[4:]:
+        load.wait()
+    for a in range(3):
+        for b in range(3):
+            kfi[a, b * chans : (b + 1) * chans] = kin[a, b].astype(F32).T.astype(BF16)
+            kfo[a, b * chans : (b + 1) * chans] = kout[a, b].astype(F32).T.astype(BF16)
 
     halo_finish(X, 0)
     for r in range(rows + 2 * HALO):
@@ -234,7 +265,7 @@
 
     CH = 2
     for r0 in range(0, rows + 2, CH):
-        acc = conv(kfi, r0, CH) + bias[...]
+        acc = conv(lambda a: kfi[a], r0, CH) + bias[...]
         pre[r0 * pitch : (r0 + CH) * pitch, :] = acc
     for r in range(rows + 2):
         v = pre[r * pitch : (r + 1) * pitch, :]
@@ -250,7 +281,7 @@
     forward.start()
 
     for r0 in range(0, rows, CH):
-        acc = conv(kfo, r0, CH)
+        acc = conv(lambda a: kfo[a], r0, CH)
         for i in range(CH):
             r = r0 + i
             state = X[top + r, left : left + width].astype(F32)
@@ -265,49 +296,68 @@
     cell_r = (lane // PW).astype(F32)
     cell_c = (lane % PW).astype(F32)
 
-    def place_slot(s, _):
-        t = s // CAP
-        k = s % CAP
-        meta = R[t, 0, k, chans : chans + META].astype(F32)
-        q = meta[2:3] + cell_c
-        target = (meta[1:2] + cell_r) * width + q + jnp.where(q >= width, float(px - width), 0.0)
-        index = lax.broadcasted_iota(jnp.int32, (2 * px, cells), 0).astype(F32)
-        E[s] = jnp.where(index == target, 1.0, 0.0).astype(BF16)
-        return 0
-
-    lax.fori_loop(0, slots, place_slot, 0)
+    def each_group(fn):
+        if slots == GROUP:
+            fn(0)
+        else:
+            lax.fori_loop(0, slots // GROUP, lambda g, _: fn(g) or 0, 0)
+
+    def place_group(g):
+        def place_rows(n, _):
+            index = lax.broadcasted_iota(jnp.int32, (width, cells), 0) + n * width
+            index = index.astype(F32)
+            for i in range(GROUP):
+                s = g * GROUP + i
+                meta = R[s // CAP, 0, s % CAP, chans : chans + META].astype(F32)
+                q = meta[2:3] + cell_c
+                target = (meta[1:2] + cell_r) * width + q
+                target = target + jnp.where(q >= width, float(px - width), 0.0)
+                E[g, pl.ds(pl.multiple_of(n * width, width), width), i * cells : (i + 1) * cells] = (
+                    jnp.where(index == target, 1.0, 0.0).astype(BF16)
+                )
+            return 0
+
+        lax.fori_loop(0, 2 * rows, place_rows, 0)
+
+    each_group(place_group)
     swap.wait()
 
-    def observe_slot(s, _):
-        t = s // CAP
-        k = s % CAP
-        patch = jnp.dot(D[0], E[s, 0:px], preferred_element_type=F32) + jnp.dot(
-            D[1], E[s, px : 2 * px], preferred_element_type=F32
-        )
-        w = jnp.concatenate([R[t, 0, k, 0:half], R[t, 1, k, 0:half]], axis=0)
-        val = jnp.concatenate([R[t, 0, k, half:chans], R[t, 1, k, half:chans]], axis=0)
-        predicted = lax.dot_general(
-            patch.astype(BF16), w, (((1,), (1,)), ((), ())), preferred_element_type=F32
-        )
-        residual = predicted - val.astype(F32)
-        inn[t, k] = jnp.where(ch == 0, residual[0:half], residual[half:chans]).astype(BF16)
-        sc = R[t, 0, k, chans : chans + META].astype(F32)[0:1]
-        weighted = (residual * sc).astype(BF16)
-        pulled_s[s] = jnp.dot(weighted, w, preferred_element_type=F32).astype(BF16)
-        return 0
-
-    lax.fori_loop(0, slots, observe_slot, 0)
-
-    GF[...] = jnp.zeros((px, chans), F32)
-
-    def spread_slot(s, _):
-        GF[...] += lax.dot_general(
-            E[s, pl.ds(pl.multiple_of(ch * px, px), px)], pulled_s[s],
+    def observe_group(g):
+        patches = jnp.dot(D[0], E[g, 0:px], preferred_element_type=F32) + jnp.dot(
+            D[1], E[g, px : 2 * px], preferred_element_type=F32
+        )
+        patches = patches.astype(BF16)
+        for i in range(GROUP):
+            s = g * GROUP + i
+            t = s // CAP
+            k = s % CAP
+            own = slice(i * cells, (i + 1) * cells)
+            w = jnp.concatenate([R[t, 0, k, 0:half], R[t, 1, k, 0:half]], axis=0)
+            val = jnp.concatenate([R[t, 0, k, half:chans], R[t, 1, k, half:chans]], axis=0)
+            predicted = lax.dot_general(
+                patches[:, own], w, (((1,), (1,)), ((), ())), preferred_element_type=F32
+            )
+            residual = predicted - val.astype(F32)
+            inn[t, k] = jnp.where(ch == 0, residual[0:half], residual[half:chans]).astype(BF16)
+            sc = R[t, 0, k, chans : chans + META].astype(F32)[0:1]
+            weighted = (residual * sc).astype(BF16)
+            pulled_s[g, :, own] = jnp.dot(weighted, w, preferred_element_type=F32).astype(BF16)
+
+    each_group(observe_group)
+
+    def spread_group(g):
+        added = lax.dot_general(
+            E[g, pl.ds(pl.multiple_of(ch * px, px), px)], pulled_s[g],
             (((1,), (1,)), ((), ())), preferred_element_type=F32,
         )
-        return 0
-
-    lax.fori_loop(0, slots, spread_slot, 0)
+        if slots == GROUP:
+            GF[...] = added
+        else:
+            GF[...] += added
+
+    if slots != GROUP:
+        GF[...] = jnp.zeros((px, chans), F32)
+    each_group(spread_group)
     for r in range(rows):
         G[top + r, left : left + width] = GF[r * width : (r + 1) * width, :].astype(BF16)
     halo_start(G, 8)
@@ -328,7 +378,7 @@
         put_row(r, G[r].astype(F32))
     for r0 in range(0, rows + 2, CH):
         part = slice(r0 * pitch, (r0 + CH) * pitch)
-        back = conv(kao, r0, CH)
+        back = conv(lambda a: mirrored(kout, a), r0, CH)
         v = pre[part, :]
         s = 1.0 / (1.0 + jnp.exp(-v))
         pre[part, :] = back * s * (1.0 + v * (1.0 - s))
@@ -339,14 +389,14 @@
             g = g * f
         put_row(r, g.astype(BF16).astype(F32))
     for r0 in range(0, rows, CH):
-        acc = conv(kai, r0, CH)
+        acc = conv(lambda a: mirrored(kin, a), r0, CH)
         for i in range(CH):
             r = r0 + i
             own = slice(r * width, (r + 1) * width)
             grad = GF[own, :] + acc[i * pitch + left : i * pitch + left + width]
             res = (base[own, :] - guide_rate * grad).T
-            out_s[0, :, own] = res[0:half]
-            out_s[1, :, own] = res[half:chans]
+            out_s[0, pl.ds(r, half, stride=rows), :] = res[0:half]
+            out_s[1, pl.ds(r, half, stride=rows), :] = res[half:chans]
     back_home = pair_copy(out_s.at[other], out_r, 3)
     back_home.start()
     out[ch] = out_s[ch]
@@ -372,41 +422,46 @@
     slots = n_lat * CAP
     pitch = width + 2 * SIDE
     px = rows * width
-    x = jnp.transpose(noisy_state.reshape(half, rows, 2, width), (2, 1, 3, 0))
-
-    def forward(k):
-        return jnp.transpose(k, (0, 1, 3, 2)).reshape(3, 3 * chans, chans)
-
-    def adjoint(k):
-        return k[::-1, ::-1].reshape(3, 3 * chans, chans)
-
     vmem = pl.BlockSpec(memory_space=pltpu.VMEM)
+    hbm = pl.BlockSpec(memory_space=pl.ANY)
     smem = pl.BlockSpec(memory_space=pltpu.SMEM)
     call = pl.pallas_call(
         functools.partial(kernel, n_lat, n_lon, rows, width, half, blocks),
         out_shape=(
-            jax.ShapeDtypeStruct((2, half, px), F32),
+            jax.ShapeDtypeStruct((2, half * rows, width), F32),
             jax.ShapeDtypeStruct((blocks, half, obs), BF16),
         ),
-        in_specs=[smem] * 3 + [vmem] * 9,
+        in_specs=[smem] * 3 + [hbm] * 3 + [vmem] + [hbm] * 3,
         out_specs=(vmem, vmem),
         scratch_shapes=[
-            pltpu.VMEM((2, rows, width, half), BF16),
+            pltpu.VMEM((half, rows, cols), BF16),
+            pltpu.VMEM((2, half * rows, width), F32),
+            pltpu.VMEM((rows, half, width), BF16),
+            pltpu.VMEM(kernel_in.shape, BF16),
+            pltpu.VMEM(kernel_out.shape, BF16),
+            pltpu.VMEM(interp_weight.shape, BF16),
+            pltpu.VMEM(observed.shape, BF16),
+            pltpu.VMEM(obs_precision.shape, BF16),
+            pltpu.VMEM(obs_precision.shape, F32),
+            pltpu.VMEM((3, 3 * chans, chans), BF16),
+            pltpu.VMEM((3, 3 * chans, chans), BF16),
+            pltpu.SemaphoreType.DMA((6,)),
+            pltpu.VMEM((2, rows, half, width), BF16),
             pltpu.VMEM((rows + 4, pitch, chans), BF16),
             pltpu.VMEM(((rows + 4) * pitch, 3 * chans), BF16),
             pltpu.VMEM(((rows + 2) * pitch, chans), F32),
             pltpu.VMEM((px, chans), F32),
             pltpu.VMEM((2, chans, px), BF16),
-            pltpu.VMEM((slots, 2 * px, cells), BF16),
+            pltpu.VMEM((slots // GROUP, 2 * px, GROUP * cells), BF16),
             pltpu.VMEM((n_lat, CAP, chans + META, obs), BF16),
             pltpu.VMEM((n_lat, 2, CAP, chans + META, obs), BF16),
             pltpu.VMEM((rows + 4, pitch, chans), BF16),
             pltpu.VMEM((px, chans), F32),
             pltpu.VMEM((n_lat, CAP, half, obs), BF16),
             pltpu.VMEM((n_lat, CAP, half, obs), BF16),
-            pltpu.VMEM((2, half, px), F32),
-            pltpu.VMEM((half, px), F32),
-            pltpu.VMEM((slots, chans, cells), BF16),
+            pltpu.VMEM((2, half * rows, width), F32),
+            pltpu.VMEM((half * rows, width), F32),
+            pltpu.VMEM((slots // GROUP, chans, GROUP * cells), BF16),
             pltpu.SMEM((blocks,), jnp.int32),
             pltpu.SemaphoreType.DMA((16,)),
             pltpu.SemaphoreType.DMA((16,)),
@@ -422,10 +477,8 @@
         ),
     )
     out, innovation = call(
-        dest_tile, row_offset, col_offset, x,
-        forward(kernel_in), forward(kernel_out), adjoint(kernel_out), adjoint(kernel_in),
-        bias_in.reshape(1, chans), interp_weight, observed,
-        obs_precision.astype(F32).reshape(blocks, 1, obs),
+        dest_tile, row_offset, col_offset, noisy_state, kernel_in, kernel_out,
+        bias_in.reshape(1, chans), interp_weight, observed, obs_precision,
     )
     next_state = jnp.transpose(out.reshape(2, half, rows, width), (1, 2, 0, 3))
     return next_state.reshape(half, rows, cols), innovation

time: 46.7 us -> 36.1 us (0.77)
  local copies, waits for them, and re-layouts: 9.24 us -> 2.54 us
  Pallas kernels: 35.9 us -> 32.7 us
  other arithmetic: 0.58 us -> 0 us
    pallas_call x1, Pallas kernels: 35.9 us -> 32.7 us  [body(): call(dest_tile, row_offset, col_offset, noisy_state, kernel_in, kernel_ou...]
    transpose x2 -> x0, local copies, waits for them, and re-layouts: 2.77 us -> none  [forward(): return jnp.transpose(k, (0, 1, 3, 2)).reshape(3, 3 * chans, chans)]
    unnamed x12 -> x3, local copies, waits for them, and re-layouts: 3.08 us -> 0.63 us
    rev x2 -> x0, local copies, waits for them, and re-layouts: 1.48 us -> none  [adjoint(): return k[::-1, ::-1].reshape(3, 3 * chans, chans)]
    reshape x1 -> x0, local copies, waits for them, and re-layouts: 1.07 us -> none  [body(): x = jnp.transpose(noisy_state.reshape(half, rows, 2, width), (2, 1, 3, 0))]
    reshape x1, local copies, waits for them, and re-layouts: 0.83 us -> 1.9 us  [body(): return (next_state.reshape(half, rows, cols), innovation)]
    reshape x1 -> x0, other arithmetic: 0.58 us -> none  [body(): obs_precision.astype(F32).reshape(blocks, 1, obs)]
where the time goes in v2:
time: 36.1 us; the launch traced here: 35.9 us
  Pallas kernels  32.7 us (91%)
  local copies, waits for them, and re-layouts  2.54 us (7%)
  between operations  0.65 us (2%)
    pallas_call x1, Pallas kernels, body(): call(dest_tile, row_offset, col_offset, noisy_state, kernel_in, kernel_ou...  32.7 us
    reshape x1, local copies, waits for them, and re-layouts, body(): return (next_state.reshape(half, rows, cols), innovation)  1.9 us

profile of v2, /device:TPU:0, one launch (start us, length us, event | category | flops | bytes accessed | tf_op | source)
XLA Modules:
  0.0 35.9 jit_solution(8231495591369847071)
XLA Ops:
  0.6 32.7 %shard_map.113 = (f32[2,512,128]{2,1,0:T(8,128)}, bf16[4,64,128]{2,1,0:T(8,128)(2,1)}) custom-call(s32[4]{0:T(128)} %dest.1, s32[4]{0:T(128)} %row_off.1, s32[4]{0:T(128)} %col_off.1, bf16[64,8,256]{2,1,0:T(8,128)(2,1)} %x_hbm.1, bf16[3,3,128,128]{3,2,1,0:T(8,128)(2,1)} %kin_hbm.1, bf16[3,3,128,128]{3,2,1,0:T(8,128)(2,1)} %kout_hbm.1, f32[1,128]{1,0:T(1,128)} %bitcast.8, ...), custom_call_target="tpu_custom_call" | custom-call | tf_op jit(solution)/shard_map/pallas_call | solution.py:479
  33.3 0.0 copy-start
  33.4 1.9 %copy_bitcast_fusion = f32[64,8,256]{2,1,0:T(8,128)} fusion(f32[2,512,128]{2,1,0:T(8,128)} %get-tuple-element.4), kind=kLoop, calls=%fused_computation | loop fusion | bytes 1048576 | tf_op jit(solution)/shard_map/reshape | solution.py:484
  35.3 0.0 copy-done
  35.3 0.6 %copy.15 = bf16[4,64,128]{2,1,0:T(8,128)(2,1)} copy(bf16[4,64,128]{2,1,0:T(8,128)(2,1)S(1)} %copy-done) | data formatting | bytes 131072
Async XLA Ops:
  33.3 1.9 %copy-start = (bf16[4,64,128]{2,1,0:T(8,128)(2,1)S(1)}, bf16[4,64,128]{2,1,0:T(8,128)(2,1)}, u32[]{:S(2)}) copy-start(bf16[4,64,128]{2,1,0:T(8,128)(2,1)} %get-tuple-element.9) | copy-start | bytes 196612

commit v3 on v2

--- a/solution.py
+++ b/solution.py
@@ -29,7 +29,7 @@
     dest, row_off, col_off, x_hbm, kin_hbm, kout_hbm, bias, weight_hbm, values_hbm, scale_hbm,
     out, inn_out,
     xv, xs, x_send, kin, kout, weight, values, scale_raw, scale, kfi, kfo, load_sem,
-    both, X, X3, pre, base, D, E, pay, R, G, GF, inn, inn_r, out_s, out_r, pulled_s,
+    both, X, X3, H3, pre, base, D, E, pay, R, G, GF, inn, inn_r, out_s, out_r, pulled_s,
     plan,
     halo_s, halo_r, pair_s, pair_r, pay_s, pay_r, inn_ss, inn_rs,
 ):
@@ -182,8 +182,8 @@
 
             guarded(dl, go)
 
-    def halo_finish(buf, base_sem):
-        for dl in (0, -1, 1):
+    def halo_finish(buf, base_sem, rows_of):
+        for dl in rows_of:
             def go(dl=dl):
                 for i, route in enumerate(routes):
                     if route[0] == dl:
@@ -197,6 +197,20 @@
             guarded(dl, go)
             guarded(-dl, got)
 
+    def rim_conv(buf, base_sem, step):
+        halo_finish(buf, base_sem, (0,))
+        for r in range(HALO, HALO + rows):
+            put_row(X3, r, buf[r].astype(F32))
+        for r0 in range(HALO, rows, CH):
+            step(r0)
+        halo_finish(buf, base_sem, (-1, 1))
+        for r in (0, 1, HALO + rows, HALO + rows + 1):
+            put_row(X3, r, buf[r].astype(F32))
+        for r0 in (0, rows):
+            step(r0)
+
+    CH = 2
+
     def clear_poles(buf):
         @pl.when(lat == 0)
         def _():
@@ -206,16 +220,16 @@
         def _():
             buf[rows + HALO : rows + 2 * HALO] = jnp.zeros((HALO, pitch, chans), BF16)
 
-    def put_row(r, v):
-        X3[r * pitch : (r + 1) * pitch, 0:chans] = pltpu.roll(v, 1, 0).astype(BF16)
-        X3[r * pitch : (r + 1) * pitch, chans : 2 * chans] = v.astype(BF16)
-        X3[r * pitch : (r + 1) * pitch, 2 * chans :] = pltpu.roll(v, pitch - 1, 0).astype(BF16)
-
-    def conv(kmat, first, count):
+    def put_row(taps, r, v):
+        taps[r * pitch : (r + 1) * pitch, 0:chans] = pltpu.roll(v, 1, 0).astype(BF16)
+        taps[r * pitch : (r + 1) * pitch, chans : 2 * chans] = v.astype(BF16)
+        taps[r * pitch : (r + 1) * pitch, 2 * chans :] = pltpu.roll(v, pitch - 1, 0).astype(BF16)
+
+    def conv(taps, kmat, first, count):
         acc = None
         for a in range(3):
             part = jnp.dot(
-                X3[(first + a) * pitch : (first + a + count) * pitch, :], kmat(a),
+                taps[(first + a) * pitch : (first + a + count) * pitch, :], kmat(a),
                 preferred_element_type=F32,
             )
             acc = part if acc is None else acc + part
@@ -259,29 +273,21 @@
             kfi[a, b * chans : (b + 1) * chans] = kin[a, b].astype(F32).T.astype(BF16)
             kfo[a, b * chans : (b + 1) * chans] = kout[a, b].astype(F32).T.astype(BF16)
 
-    halo_finish(X, 0)
-    for r in range(rows + 2 * HALO):
-        put_row(r, X[r].astype(F32))
-
-    CH = 2
-    for r0 in range(0, rows + 2, CH):
-        acc = conv(lambda a: kfi[a], r0, CH) + bias[...]
+    def hidden_rows(r0):
+        acc = conv(X3, lambda a: kfi[a], r0, CH) + bias[...]
         pre[r0 * pitch : (r0 + CH) * pitch, :] = acc
-    for r in range(rows + 2):
-        v = pre[r * pitch : (r + 1) * pitch, :]
-        h = v / (1.0 + jnp.exp(-v))
-        f = edge_factor(r)
-        if f is not None:
-            h = h * f
-        put_row(r, h.astype(BF16).astype(F32))
-
-    for step in range(1, n_lat):
-        pay_copy(step - 1, step).wait()
-    forward = pair_copy(R.at[:, ch], R.at[:, ch], 1)
-    forward.start()
+        h = acc / (1.0 + jnp.exp(-acc))
+        for i in range(CH):
+            row = h[i * pitch : (i + 1) * pitch]
+            f = edge_factor(r0 + i)
+            if f is not None:
+                row = row * f
+            put_row(H3, r0 + i, row.astype(BF16).astype(F32))
+
+    rim_conv(X, 0, hidden_rows)
 
     for r0 in range(0, rows, CH):
-        acc = conv(lambda a: kfo[a], r0, CH)
+        acc = conv(H3, lambda a: kfo[a], r0, CH)
         for i in range(CH):
             r = r0 + i
             state = X[top + r, left : left + width].astype(F32)
@@ -291,7 +297,11 @@
     swap = pair_copy(D.at[ch], D.at[ch], 2)
     swap.start()
 
-    forward.wait()
+    for step in range(1, n_lat):
+        pay_copy(step - 1, step).wait()
+    forward = pair_copy(R.at[:, ch], R.at[:, ch], 1)
+    forward.start()
+
     lane = lax.broadcasted_iota(jnp.int32, (1, cells), 1)
     cell_r = (lane // PW).astype(F32)
     cell_c = (lane % PW).astype(F32)
@@ -308,7 +318,7 @@
             index = index.astype(F32)
             for i in range(GROUP):
                 s = g * GROUP + i
-                meta = R[s // CAP, 0, s % CAP, chans : chans + META].astype(F32)
+                meta = R[s // CAP, ch, s % CAP, chans : chans + META].astype(F32)
                 q = meta[2:3] + cell_c
                 target = (meta[1:2] + cell_r) * width + q
                 target = target + jnp.where(q >= width, float(px - width), 0.0)
@@ -320,6 +330,7 @@
         lax.fori_loop(0, 2 * rows, place_rows, 0)
 
     each_group(place_group)
+    forward.wait()
     swap.wait()
 
     def observe_group(g):
@@ -373,23 +384,22 @@
     for step in range(1, n_lat):
         inn_copy(step - 1, step).start()
     inn_r[lat] = inn[lat]
-    halo_finish(G, 8)
-    for r in range(rows + 2 * HALO):
-        put_row(r, G[r].astype(F32))
-    for r0 in range(0, rows + 2, CH):
-        part = slice(r0 * pitch, (r0 + CH) * pitch)
-        back = conv(lambda a: mirrored(kout, a), r0, CH)
-        v = pre[part, :]
+
+    def grad_rows(r0):
+        back = conv(X3, lambda a: mirrored(kout, a), r0, CH)
+        v = pre[r0 * pitch : (r0 + CH) * pitch, :]
         s = 1.0 / (1.0 + jnp.exp(-v))
-        pre[part, :] = back * s * (1.0 + v * (1.0 - s))
-    for r in range(rows + 2):
-        g = pre[r * pitch : (r + 1) * pitch, :]
-        f = edge_factor(r)
-        if f is not None:
-            g = g * f
-        put_row(r, g.astype(BF16).astype(F32))
+        g = back * s * (1.0 + v * (1.0 - s))
+        for i in range(CH):
+            row = g[i * pitch : (i + 1) * pitch]
+            f = edge_factor(r0 + i)
+            if f is not None:
+                row = row * f
+            put_row(H3, r0 + i, row.astype(BF16).astype(F32))
+
+    rim_conv(G, 8, grad_rows)
     for r0 in range(0, rows, CH):
-        acc = conv(lambda a: mirrored(kin, a), r0, CH)
+        acc = conv(H3, lambda a: mirrored(kin, a), r0, CH)
         for i in range(CH):
             r = r0 + i
             own = slice(r * width, (r + 1) * width)
@@ -423,7 +433,7 @@
     pitch = width + 2 * SIDE
     px = rows * width
     vmem = pl.BlockSpec(memory_space=pltpu.VMEM)
-    hbm = pl.BlockSpec(memory_space=pl.ANY)
+    hbm = pl.BlockSpec(memory_space=pltpu.HBM)
     smem = pl.BlockSpec(memory_space=pltpu.SMEM)
     call = pl.pallas_call(
         functools.partial(kernel, n_lat, n_lon, rows, width, half, blocks),
@@ -449,6 +459,7 @@
             pltpu.VMEM((2, rows, half, width), BF16),
             pltpu.VMEM((rows + 4, pitch, chans), BF16),
             pltpu.VMEM(((rows + 4) * pitch, 3 * chans), BF16),
+            pltpu.VMEM(((rows + 2) * pitch, 3 * chans), BF16),
             pltpu.VMEM(((rows + 2) * pitch, chans), F32),
             pltpu.VMEM((px, chans), F32),
             pltpu.VMEM((2, chans, px), BF16),

time: 36.1 us -> 33.7 us (0.934)
  Pallas kernels: 32.7 us -> 30.4 us
    pallas_call x1, Pallas kernels: 32.7 us -> 30.4 us  [body(): call(dest_tile, row_offset, col_offset, noisy_state, kernel_in, kernel_ou...]
where the time goes in v3:
time: 33.7 us; the launch traced here: 33.5 us
  Pallas kernels  30.4 us (90%)
  local copies, waits for them, and re-layouts  2.54 us (8%)
  between operations  0.65 us (2%)
    pallas_call x1, Pallas kernels, body(): call(dest_tile, row_offset, col_offset, noisy_state, kernel_in, kernel_ou...  30.4 us
    reshape x1, local copies, waits for them, and re-layouts, body(): return (next_state.reshape(half, rows, cols), innovation)  1.9 us

profile of v3, /device:TPU:0, one launch (start us, length us, event | category | flops | bytes accessed | tf_op | source)
XLA Modules:
  0.0 33.5 jit_solution(7344584588324291435)
XLA Ops:
  0.6 30.4 %shard_map.113 = (f32[2,512,128]{2,1,0:T(8,128)}, bf16[4,64,128]{2,1,0:T(8,128)(2,1)}) custom-call(s32[4]{0:T(128)} %dest.1, s32[4]{0:T(128)} %row_off.1, s32[4]{0:T(128)} %col_off.1, bf16[64,8,256]{2,1,0:T(8,128)(2,1)} %x_hbm.1, bf16[3,3,128,128]{3,2,1,0:T(8,128)(2,1)} %kin_hbm.1, bf16[3,3,128,128]{3,2,1,0:T(8,128)(2,1)} %kout_hbm.1, f32[1,128]{1,0:T(1,128)} %bitcast.8, ...), custom_call_target="tpu_custom_call" | custom-call | tf_op jit(solution)/shard_map/pallas_call | solution.py:490
  31.0 0.0 copy-start
  31.0 1.9 %copy_bitcast_fusion = f32[64,8,256]{2,1,0:T(8,128)} fusion(f32[2,512,128]{2,1,0:T(8,128)} %get-tuple-element.4), kind=kLoop, calls=%fused_computation | loop fusion | bytes 1048576 | tf_op jit(solution)/shard_map/reshape | solution.py:495
  32.9 0.0 copy-done
  32.9 0.6 %copy.15 = bf16[4,64,128]{2,1,0:T(8,128)(2,1)} copy(bf16[4,64,128]{2,1,0:T(8,128)(2,1)S(1)} %copy-done) | data formatting | bytes 131072
Async XLA Ops:
  31.0 1.9 %copy-start = (bf16[4,64,128]{2,1,0:T(8,128)(2,1)S(1)}, bf16[4,64,128]{2,1,0:T(8,128)(2,1)}, u32[]{:S(2)}) copy-start(bf16[4,64,128]{2,1,0:T(8,128)(2,1)} %get-tuple-element.9) | copy-start | bytes 196612
